TPU v7x, 32 devices: a whole 2x2x4 slice. The times are simulated.
32 devices in a mesh: groups: 2 (over x), shard: 16 (over z, y, core).
Axes of the slice: x: 2, y: 2, z: 4, core: 2. Of those that a mesh axis runs over, the one named last changes fastest.
Arguments:
- echoes: float32 [1, 2, 4, 512, 8192], P(None, None, 'groups', 'shard'), parts along dimension 2, may hold values from -6 to 6
- waveform: float32 [2, 8192], replicated, may hold values from -6 to 6
- doppler_taper: float32 [512], replicated, may hold values from 0.3 to 1
- cfar_guard: int32 [4], P('groups'), parts along dimension 0, may hold values from 1 to 4, as said below
- cfar_train: int32 [4], P('groups'), parts along dimension 0, may hold values from 2 to 16
- noise_floor: float32 [4], P('groups'), parts along dimension 0, may hold values from 0.5 to 2
Outputs:
- cfar_ratio: float32 [1, 4, 512, 8192], P(None, 'groups', None, 'shard'), parts along dimension 1
There are 2 independent parts, one for each index of `groups`. A program takes and returns all parts, laid end to end along the dimension named above; an argument that names none is the same for every part. Nothing has to cross between parts.
Inputs may be any that keep to these rules, and one draw needn't show every extreme that they name: In every draw some beam has cfar_guard 4 together with cfar_train 16; no beam has more of either.
All inputs are finite; a program needn't handle non-finite values.
Results may differ from a plain program's by a relative error of at most 0.000075.
Values sent between devices are 32-bit elements; how exact they have to be, the bound alone decides.
A program may use at most 64 MiB of HBM per device.

v0:
```python
import functools
import math

import jax
import jax.numpy as jnp
import numpy as np
from jax import lax
from jax.experimental import pallas as pl
from jax.experimental.pallas import tpu as pltpu
from jax.sharding import PartitionSpec as P

GB = 128
ROWS = 8
EDGE = 24
MESH = pl.DeviceIdType.MESH


def split(table):
    table = np.asarray(table, np.float32)
    high = table.astype(jnp.bfloat16)
    low = (table - high.astype(np.float32)).astype(jnp.bfloat16)
    return high, low


def dft(length, size=None):
    size = size or length
    i = np.arange(size)[:, None] * np.arange(length)[None, :] % length
    angles = 2.0 * np.pi / length * i
    return np.cos(angles), np.sin(angles)


def tables(gates, pulses):
    ga = gates // GB
    ca, sa = dft(ga)
    cb, sb = dft(GB)

    def left(matrix):
        high, low = split(matrix)
        return np.block([[high, high], [low, np.zeros_like(low)]])

    first = left(np.block([[ca, sa], [-sa, ca]]))
    last = left(np.block([[ca, -sa], [sa, ca]]))
    per = GB // ga
    c = np.arange(GB).reshape(GB // per, per).T.reshape(-1)
    cb, sb = cb[:, c], sb[:, c]
    second = np.stack(split(np.block([[cb, -sb], [sb, cb]])))
    third = np.stack(split(np.block([[cb.T, sb.T], [-sb.T, cb.T]])))
    i = np.arange(ga)[:, None] * np.arange(GB)[None, :] % gates
    twiddle = np.stack([np.cos(2 * np.pi / gates * i), np.sin(2 * np.pi / gates * i)])
    half = pulses // 2
    cp, sp = dft(pulses)
    doppler = [
        np.stack(split(np.concatenate([cp[e::2, :half], sp[e::2, :half]], axis=0))) for e in range(2)
    ]
    return first, second, third, last, twiddle.astype(np.float32), np.stack(doppler)


def parts(x):
    high = x.astype(jnp.bfloat16)
    low = (x - high.astype(jnp.float32)).astype(jnp.bfloat16)
    return high, low


def dot(a, b):
    return jnp.dot(a, b, preferred_element_type=jnp.float32)


def kernel(
    n, beams, pulses, gates,
    echoes, waveform, taper, first, second, third, last, twiddle, doppler_hbm,
    power_out, halo_out,
    xin, xs, wave, filt, sent, got, table, rhs, spec, power, edge, halo, border,
    in_sem, table_sem, send_sem, recv_sem, edge_send, edge_recv, power_sem, halo_sem,
):
    me = lax.axis_index("shard")
    ga = gates // GB
    tiles = ga // n
    groups = pulses // n // ROWS
    order = sorted(range(1, n), key=lambda k: (abs(2 * k - n), k))

    def load(b, pg):
        start = pg * ROWS if isinstance(pg, int) else pl.multiple_of(pg * ROWS, ROWS)
        return pltpu.make_async_copy(
            echoes.at[0, :, b, pl.ds(start, ROWS), :], xin.at[b, pg], in_sem.at[b, pg]
        )

    for b in range(beams):
        for pg in range(groups):
            load(b, pg).start()
    table_copy = pltpu.make_async_copy(doppler_hbm, table, table_sem)

    barrier = pltpu.get_barrier_semaphore()
    for k in order:
        pl.semaphore_signal(
            barrier, inc=1, device_id={"shard": lax.rem(me + k, n)}, device_id_type=MESH
        )

    per = GB // ga
    scale = 1.0 / (gates * math.sqrt(pulses))
    for c in range(2):
        for m in range(ga):
            wave[m:m + 1, :] = waveform[c:c + 1, m * GB:(m + 1) * GB]
        lines = wave[...] * scale
        turned = [lines] + [pltpu.roll(lines, GB - h * ga, axis=1) for h in range(1, per)]
        filt[c] = jnp.concatenate(turned, axis=0).T[:ga]

    def stacked(ref):
        return jnp.concatenate([ref[0], ref[0], ref[1]], axis=0)

    def compress(b, pg):
        load(b, pg).wait()
        for c in range(2):
            for i in range(ga):
                xs[c, i * ROWS:(i + 1) * ROWS, :] = xin[b, pg, c, :, i * GB:(i + 1) * GB]
        tc, ts = twiddle[0], twiddle[1]
        lhs = []
        for p in range(0, ROWS, 2):
            x = jnp.concatenate(
                [
                    jnp.concatenate([xs[c, pl.ds(p + e, ga, stride=ROWS), :] for c in range(2)], axis=0)
                    for e in range(2)
                ],
                axis=1,
            )
            y = dot(first[...], jnp.concatenate(parts(x), axis=0))
            y = y[:2 * ga] + y[2 * ga:]
            for e in range(2):
                yr, yi = y[:ga, e * GB:(e + 1) * GB], y[ga:, e * GB:(e + 1) * GB]
                z = jnp.concatenate([yr * tc + yi * ts, yi * tc - yr * ts], axis=1)
                high, low = parts(z)
                lhs.append(jnp.concatenate([high, low, high], axis=1))
        x = dot(jnp.concatenate(lhs, axis=0), stacked(second))
        lhs = []
        fr, fi = filt[0], filt[1]
        for p in range(ROWS):
            weight = taper[(me * groups + pg) * ROWS + p]
            hr, hi = fr * weight, fi * weight
            xr, xi = x[p * ga:(p + 1) * ga, :GB], x[p * ga:(p + 1) * ga, GB:]
            z = jnp.concatenate([xr * hr + xi * hi, xi * hr - xr * hi], axis=1)
            high, low = parts(z)
            lhs.append(jnp.concatenate([high, low, high], axis=1))
        x = dot(jnp.concatenate(lhs, axis=0), stacked(third))
        for p in range(0, ROWS, 2):
            pair = []
            for e in range(2):
                r = (p + e) * ga
                xr, xi = x[r:r + ga, :GB], x[r:r + ga, GB:]
                pair.append(jnp.concatenate([xr * tc - xi * ts, xi * tc + xr * ts], axis=0))
            y = dot(last[...], jnp.concatenate(parts(jnp.concatenate(pair, axis=1)), axis=0))
            y = y[:2 * ga] + y[2 * ga:]
            for e in range(2):
                for c in range(2):
                    sent.at[b, c, pg].reshape(ga * ROWS, GB)[pl.ds(p + e, ga, stride=ROWS), :] = y[
                        c * ga:(c + 1) * ga, e * GB:(e + 1) * GB
                    ]

    def send_group(b, pg):
        dst = got.at[b, :, :, me * groups + pg]
        for k in order:
            to = lax.rem(me + k, n)
            pltpu.make_async_remote_copy(
                src_ref=sent.at[b, :, pg, pl.ds(to * tiles, tiles)],
                dst_ref=dst,
                send_sem=send_sem.at[b],
                recv_sem=recv_sem.at[b, 0],
                device_id={"shard": to},
                device_id_type=MESH,
            ).start()
        pltpu.make_async_copy(
            sent.at[b, :, pg, pl.ds(me * tiles, tiles)], dst, recv_sem.at[b, 0]
        ).start()

    def send_tile(b, j):
        dst = got.at[b, :, j, pl.ds(me * groups, groups)]
        for k in order:
            to = lax.rem(me + k, n)
            pltpu.make_async_remote_copy(
                src_ref=sent.at[b, :, :, to * tiles + j],
                dst_ref=dst,
                send_sem=send_sem.at[b],
                recv_sem=recv_sem.at[b, j],
                device_id={"shard": to},
                device_id_type=MESH,
            ).start()
        pltpu.make_async_copy(sent.at[b, :, :, me * tiles + j], dst, recv_sem.at[b, j]).start()

    for b in range(beams):
        final = b == beams - 1

        @pl.loop(0, groups)
        def _(pg):
            compress(b, pg)
            if b == 0:
                @pl.when(pg == 0)
                def _():
                    table_copy.start()
                    pl.semaphore_wait(barrier, n - 1)

            if not final:
                send_group(b, pg)

        if final:
            @pl.loop(0, tiles)
            def _(t):
                send_tile(b, lax.rem(t * (tiles - 1), tiles))

    table_copy.wait()

    half = pulses // 2

    def transform(b, j):
        x = jnp.concatenate([got[b, c, j].reshape(pulses, GB) for c in range(2)], axis=1)
        for e, y in enumerate((x[:half] + x[half:], x[:half] - x[half:])):
            high, low = parts(y)
            rhs[e, 0:half] = high
            rhs[e, half:2 * half] = low
            rhs[e, 2 * half:] = high
        for e in range(2):
            lhs = jnp.concatenate([table[e, 0], table[e, 0], table[e, 1]], axis=1)
            spec[e] = dot(lhs, rhs[e])
            re = spec[e, :half, :GB] + spec[e, half:, GB:]
            im = spec[e, :half, GB:] - spec[e, half:, :GB]
            power.at[b, j][pl.ds(e, half, stride=2), :] = re * re + im * im
        put(b, j).start()

    def put(b, j):
        return pltpu.make_async_copy(power.at[b, j], power_out.at[b, j], power_sem.at[b, j])

    def put_halo(b):
        return pltpu.make_async_copy(border.at[b], halo_out.at[b], halo_sem.at[b])

    def edge_copy(b, side):
        to = lax.rem(me + (n - 1 if side == 0 else 1), n)
        return pltpu.make_async_remote_copy(
            src_ref=edge.at[b, side],
            dst_ref=halo.at[b, side],
            send_sem=edge_send.at[b, side],
            recv_sem=edge_recv.at[b, side],
            device_id={"shard": to},
            device_id_type=MESH,
        )

    def send_edges(b):
        edge[b, 0] = power[b, 0].T[:EDGE]
        edge[b, 1] = power[b, tiles - 1].T[GB - EDGE:]
        for side in range(2):
            edge_copy(b, side).start()

    def take_edges(b):
        for side in range(2):
            edge_copy(b, side).wait()
        border[b, 0] = jnp.where(me < n - 1, halo[b, 0], 0.0)
        border[b, 1] = jnp.where(me > 0, halo[b, 1], 0.0)
        put_halo(b).start()

    for b in range(beams - 1):
        pltpu.make_async_copy(got.at[b], got.at[b], recv_sem.at[b, 0]).wait()

        @pl.loop(0, tiles)
        def _(j):
            transform(b, j)

        send_edges(b)

    b = beams - 1
    for t in range(tiles):
        j = t * (tiles - 1) % tiles
        arrived = got.at[b, :, j]
        pltpu.make_async_copy(arrived, arrived, recv_sem.at[b, j]).wait()
        transform(b, j)
        if t == min(1, tiles - 1):
            send_edges(b)
        if t == max(tiles - 2, min(1, tiles - 1)):
            for i in range(beams):
                take_edges(i)

    for b in range(beams):
        whole = sent.at[b, :, :, pl.ds(0, (n - 1) * tiles)]
        pltpu.make_async_copy(whole, whole, send_sem.at[b]).wait()
        put_halo(b).wait()
        for j in range(tiles):
            put(b, j).wait()


def cfar_kernel(guard, train, floor, power, halo, out):
    b = pl.program_id(0)
    tiles, rows = power.shape[1:3]
    m = lax.broadcasted_iota(jnp.int32, (3 * GB, GB), 0) - GB
    k = lax.broadcasted_iota(jnp.int32, (3 * GB, GB), 1)
    apart = jnp.abs(m - k)
    inside = (apart > guard[b]) & (apart <= guard[b] + train[b])
    band = jnp.where(inside, 1.0, 0.0).astype(jnp.bfloat16)
    band = jnp.concatenate([band, band], axis=0)
    zeros = jnp.zeros((GB - EDGE, rows), jnp.float32)
    after = jnp.concatenate([halo[0, 0], zeros], axis=0).T
    before = jnp.concatenate([zeros, halo[0, 1]], axis=0).T
    twice = 2.0 * train[b].astype(jnp.float32)
    base = floor[b] * twice
    cells = [before] + [power[0, j] for j in range(tiles)] + [after]
    cells = [(x, *parts(x)) for x in cells]
    for j in range(tiles):
        near = cells[j:j + 3]
        total = dot(jnp.concatenate([x[1] for x in near] + [x[2] for x in near], axis=1), band)
        out[0, 0, :, j * GB:(j + 1) * GB] = near[1][0] * twice / (base + total)


def solution(mesh):
    n = mesh.shape["shard"]

    def step(echoes, waveform, doppler_taper, cfar_guard, cfar_train, noise_floor):
        beams, local, gates = echoes.shape[2:]
        pulses = local * n
        ga = gates // GB
        tiles = ga // n
        groups = local // ROWS
        consts = tables(gates, pulses)
        vmem = pl.BlockSpec(memory_space=pltpu.VMEM)
        smem = pl.BlockSpec(memory_space=pltpu.SMEM)
        hbm = pl.BlockSpec(memory_space=pltpu.HBM)
        f32, bf16 = jnp.float32, jnp.bfloat16
        dma = pltpu.SemaphoreType.DMA
        power, halo = pl.pallas_call(
            functools.partial(kernel, n, beams, pulses, gates),
            out_shape=(
                jax.ShapeDtypeStruct((beams, tiles, pulses, GB), f32),
                jax.ShapeDtypeStruct((beams, 2, EDGE, pulses), f32),
            ),
            in_specs=[hbm, vmem, smem, vmem, vmem, vmem, vmem, vmem, hbm],
            out_specs=(hbm, hbm),
            scratch_shapes=[
                pltpu.VMEM((beams, groups, 2, ROWS, gates), f32),
                pltpu.VMEM((2, ga * ROWS, GB), f32),
                pltpu.VMEM((ga, GB), f32),
                pltpu.VMEM((2, ga, GB), f32),
                pltpu.VMEM((beams, 2, groups, ga, ROWS, GB), f32),
                pltpu.VMEM((beams, 2, tiles, pulses // ROWS, ROWS, GB), f32),
                pltpu.VMEM((2, 2, pulses, pulses // 2), bf16),
                pltpu.VMEM((2, 3 * pulses // 2, 2 * GB), bf16),
                pltpu.VMEM((2, pulses, 2 * GB), f32),
                pltpu.VMEM((beams, tiles, pulses, GB), f32),
                pltpu.VMEM((beams, 2, EDGE, pulses), f32),
                pltpu.VMEM((beams, 2, EDGE, pulses), f32),
                pltpu.VMEM((beams, 2, EDGE, pulses), f32),
                dma((beams, groups)),
                dma,
                dma((beams,)),
                dma((beams, tiles)),
                dma((beams, 2)),
                dma((beams, 2)),
                dma((beams, tiles)),
                dma((beams,)),
            ],
            compiler_params=pltpu.CompilerParams(
                collective_id=0, has_side_effects=True, vmem_limit_bytes=60000 * 1024
            ),
        )(echoes, waveform, doppler_taper, *(jnp.asarray(c) for c in consts))
        cut = pulses // 2
        return pl.pallas_call(
            cfar_kernel,
            grid=(beams, pulses // cut),
            out_shape=jax.ShapeDtypeStruct((1, beams, pulses, gates // n), f32),
            in_specs=[
                smem, smem, smem,
                pl.BlockSpec((1, tiles, cut, GB), lambda b, q: (b, 0, q, 0)),
                pl.BlockSpec((1, 2, EDGE, cut), lambda b, q: (b, 0, 0, q)),
            ],
            out_specs=pl.BlockSpec((1, 1, cut, tiles * GB), lambda b, q: (0, b, q, 0)),
            compiler_params=pltpu.CompilerParams(vmem_limit_bytes=60000 * 1024),
        )(cfar_guard, cfar_train, noise_floor, power, halo)

    in_specs = (
        P(None, None, "groups", "shard", None),
        P(),
        P(),
        P("groups"),
        P("groups"),
        P("groups"),
    )
    return jax.shard_map(
        step, mesh=mesh, in_specs=in_specs, out_specs=P(None, "groups", None, "shard"), check_vma=False
    )
```

profile of v0, /device:TPU:9, one launch (start us, length us, event | category | flops | bytes accessed | tf_op | source)
XLA Modules:
  0.0 103.9 jit_solution(93470406408403417)
XLA Ops:
  0.0 98.8 %shard_map.118 = (f32[2,4,512,128]{3,2,1,0:T(8,128)}, f32[2,2,24,512]{3,2,1,0:T(8,128)}) custom-call(f32[1,2,2,32,8192]{4,3,2,1,0:T(8,128)} %echoes.1, f32[2,8192]{1,0:T(2,128)} %waveform.1, f32[512]{0:T(512)} %taper.1, bf16[256,256]{1,0:T(8,128)(2,1)} %constant.12.clone.first, bf16[2,256,256]{2,1,0:T(8,128)(2,1)} %constant.13.clone.second, ...), custom_call_target="tpu_custom_call" | custom-call | tf_op jit(solution)/shard_map/pallas_call | solution.py:322
  98.8 5.1 %shard_map.119 = f32[1,2,512,512]{3,2,1,0:T(8,128)} custom-call(s32[2]{0:T(128)} %guard.1, s32[2]{0:T(128)} %train.1, f32[2]{0:T(128)} %floor.1, f32[2,4,512,128]{3,2,1,0:T(8,128)} %get-tuple-element.7.power, f32[2,2,24,512]{3,2,1,0:T(8,128)} %get-tuple-element.8.halo), custom_call_target="tpu_custom_call" | custom-call | tf_op jit(solution)/shard_map/pallas_call | solution.py:358
where the time goes:
time: 105 us; the launch traced here: 104 us
  Pallas kernels  104 us (99%)
    pallas_call x1, Pallas kernels, step(): pl.pallas_call(functools.partial(kernel, n, beams, pulses, gates), out_sh...  98.8 us
    pallas_call x1, Pallas kernels, step(): pl.pallas_call(cfar_kernel, grid=(beams, pulses // cut), out_shape=jax.Sh...  5.1 us

commit v1 on v0

--- a/solution.py
+++ b/solution.py
@@ -67,16 +67,25 @@
 
 def kernel(
     n, beams, pulses, gates,
-    echoes, waveform, taper, first, second, third, last, twiddle, doppler_hbm,
-    power_out, halo_out,
-    xin, xs, wave, filt, sent, got, table, rhs, spec, power, edge, halo, border,
-    in_sem, table_sem, send_sem, recv_sem, edge_send, edge_recv, power_sem, halo_sem,
+    echoes, waveform_hbm, taper_hbm, guard_hbm, train_hbm, floor_hbm,
+    first_hbm, second_hbm, third_hbm, last_hbm, twiddle_hbm, doppler_hbm,
+    out,
+    xin, xs, wave, filt, sent, got, table, rhs, power, own, cross, edge, halo, band,
+    waveform, taper, guard, train, floor, first, second, third, last, twiddle,
+    in_sem, small_sem, table_sem, send_sem, recv_sem, edge_send, edge_recv,
 ):
     me = lax.axis_index("shard")
     ga = gates // GB
     tiles = ga // n
     groups = pulses // n // ROWS
+    half = pulses // 2
     order = sorted(range(1, n), key=lambda k: (abs(2 * k - n), k))
+
+    barrier = pltpu.get_barrier_semaphore()
+    for k in order:
+        pl.semaphore_signal(
+            barrier, inc=1, device_id={"shard": lax.rem(me + k, n)}, device_id_type=MESH
+        )
 
     def load(b, pg):
         start = pg * ROWS if isinstance(pg, int) else pl.multiple_of(pg * ROWS, ROWS)
@@ -84,25 +93,38 @@
             echoes.at[0, :, b, pl.ds(start, ROWS), :], xin.at[b, pg], in_sem.at[b, pg]
         )
 
+    small = [
+        pltpu.make_async_copy(src, dst, small_sem.at[i])
+        for i, (src, dst) in enumerate(
+            (
+                (waveform_hbm, waveform), (taper_hbm, taper), (first_hbm, first),
+                (twiddle_hbm, twiddle), (second_hbm, second), (third_hbm, third), (last_hbm, last),
+                (guard_hbm, guard), (train_hbm, train), (floor_hbm, floor),
+            )
+        )
+    ]
+    table_copy = pltpu.make_async_copy(doppler_hbm, table, table_sem)
+    small[0].start()
+    load(0, 0).start()
+    for copy in small[1:]:
+        copy.start()
     for b in range(beams):
         for pg in range(groups):
-            load(b, pg).start()
-    table_copy = pltpu.make_async_copy(doppler_hbm, table, table_sem)
-
-    barrier = pltpu.get_barrier_semaphore()
-    for k in order:
-        pl.semaphore_signal(
-            barrier, inc=1, device_id={"shard": lax.rem(me + k, n)}, device_id_type=MESH
-        )
+            if b or pg:
+                load(b, pg).start()
+    table_copy.start()
 
     per = GB // ga
     scale = 1.0 / (gates * math.sqrt(pulses))
+    small[0].wait()
     for c in range(2):
         for m in range(ga):
             wave[m:m + 1, :] = waveform[c:c + 1, m * GB:(m + 1) * GB]
         lines = wave[...] * scale
         turned = [lines] + [pltpu.roll(lines, GB - h * ga, axis=1) for h in range(1, per)]
         filt[c] = jnp.concatenate(turned, axis=0).T[:ga]
+    for copy in small[1:]:
+        copy.wait()
 
     def stacked(ref):
         return jnp.concatenate([ref[0], ref[0], ref[1]], axis=0)
@@ -193,7 +215,6 @@
             if b == 0:
                 @pl.when(pg == 0)
                 def _():
-                    table_copy.start()
                     pl.semaphore_wait(barrier, n - 1)
 
             if not final:
@@ -206,9 +227,19 @@
 
     table_copy.wait()
 
-    half = pulses // 2
-
-    def transform(b, j):
+    m = lax.broadcasted_iota(jnp.int32, (GB, 2 * GB), 0)
+    k = lax.broadcasted_iota(jnp.int32, (GB, 2 * GB), 1)
+    apart = jnp.where(k < GB, jnp.abs(m - k), jnp.where(k < GB + GB // 2, k - m, m + 2 * GB - k))
+    for b in range(beams):
+        inside = (apart > guard[b]) & (apart <= guard[b] + train[b])
+        lines = jnp.where(inside, 1.0, 0.0).astype(jnp.bfloat16)
+        band[b, :GB] = lines
+        band[b, GB:] = lines
+
+    def sums(b, x):
+        return dot(jnp.concatenate(parts(x), axis=1), band[b])
+
+    def transform(b, j, then=None):
         x = jnp.concatenate([got[b, c, j].reshape(pulses, GB) for c in range(2)], axis=1)
         for e, y in enumerate((x[:half] + x[half:], x[:half] - x[half:])):
             high, low = parts(y)
@@ -217,17 +248,23 @@
             rhs[e, 2 * half:] = high
         for e in range(2):
             lhs = jnp.concatenate([table[e, 0], table[e, 0], table[e, 1]], axis=1)
-            spec[e] = dot(lhs, rhs[e])
-            re = spec[e, :half, :GB] + spec[e, half:, GB:]
-            im = spec[e, :half, GB:] - spec[e, half:, :GB]
-            power.at[b, j][pl.ds(e, half, stride=2), :] = re * re + im * im
-        put(b, j).start()
-
-    def put(b, j):
-        return pltpu.make_async_copy(power.at[b, j], power_out.at[b, j], power_sem.at[b, j])
-
-    def put_halo(b):
-        return pltpu.make_async_copy(border.at[b], halo_out.at[b], halo_sem.at[b])
+            spec = dot(lhs, rhs[e])
+            re = spec[:half, :GB] + spec[half:, GB:]
+            im = spec[:half, GB:] - spec[half:, :GB]
+            p = re * re + im * im
+            power[b, j, e] = p
+            total = sums(b, p)
+            own[b, j, e] = total[:, :GB]
+            cross[b, j + 1, e] = total[:, GB:]
+            if then is not None:
+                then(e)
+
+    def ratio(b, j, e):
+        lower = lax.broadcasted_iota(jnp.int32, (half, GB), 1) < GB // 2
+        twice = 2.0 * train[b].astype(jnp.float32)
+        base = floor[b] * twice
+        total = own[b, j, e] + jnp.where(lower, cross[b, j, e], cross[b, j + 2, e])
+        out.at[b, j][pl.ds(e, half, stride=2), :] = power[b, j, e] * twice / (base + total)
 
     def edge_copy(b, side):
         to = lax.rem(me + (n - 1 if side == 0 else 1), n)
@@ -241,17 +278,25 @@
         )
 
     def send_edges(b):
-        edge[b, 0] = power[b, 0].T[:EDGE]
-        edge[b, 1] = power[b, tiles - 1].T[GB - EDGE:]
+        for e in range(2):
+            rows = slice(e * half, (e + 1) * half)
+            edge[b, 0, :, rows] = power[b, 0, e].T[:EDGE]
+            edge[b, 1, :, rows] = power[b, tiles - 1, e].T[GB - EDGE:]
         for side in range(2):
             edge_copy(b, side).start()
 
     def take_edges(b):
         for side in range(2):
             edge_copy(b, side).wait()
-        border[b, 0] = jnp.where(me < n - 1, halo[b, 0], 0.0)
-        border[b, 1] = jnp.where(me > 0, halo[b, 1], 0.0)
-        put_halo(b).start()
+        after = jnp.where(me < n - 1, halo[b, 0], 0.0)
+        before = jnp.where(me > 0, halo[b, 1], 0.0)
+        zeros = jnp.zeros((GB - 2 * EDGE, half), jnp.float32)
+        for e in range(2):
+            rows = slice(e * half, (e + 1) * half)
+            x = jnp.concatenate([after[:, rows], zeros, before[:, rows]], axis=0).T
+            total = sums(b, x)[:, GB:]
+            cross[b, 0, e] = total
+            cross[b, tiles + 1, e] = total
 
     for b in range(beams - 1):
         pltpu.make_async_copy(got.at[b], got.at[b], recv_sem.at[b, 0]).wait()
@@ -263,45 +308,50 @@
         send_edges(b)
 
     b = beams - 1
+    done = set()
+    ready = set()
+
+    def ratios(e):
+        for j in range(tiles):
+            if j not in done and {j - 1, j, j + 1} & set(range(tiles)) <= ready:
+                ratio(b, j, e)
+                if e == 1:
+                    done.add(j)
+
     for t in range(tiles):
         j = t * (tiles - 1) % tiles
         arrived = got.at[b, :, j]
         pltpu.make_async_copy(arrived, arrived, recv_sem.at[b, j]).wait()
-        transform(b, j)
+        ready.add(j)
+        transform(b, j, ratios if 2 < tiles == t + 1 else None)
         if t == min(1, tiles - 1):
             send_edges(b)
         if t == max(tiles - 2, min(1, tiles - 1)):
             for i in range(beams):
                 take_edges(i)
+            for i in range(beams - 1):
+                for jj in range(tiles):
+                    for e in range(2):
+                        ratio(i, jj, e)
+            for e in range(2):
+                ratios(e)
 
     for b in range(beams):
         whole = sent.at[b, :, :, pl.ds(0, (n - 1) * tiles)]
         pltpu.make_async_copy(whole, whole, send_sem.at[b]).wait()
-        put_halo(b).wait()
-        for j in range(tiles):
-            put(b, j).wait()
-
-
-def cfar_kernel(guard, train, floor, power, halo, out):
-    b = pl.program_id(0)
-    tiles, rows = power.shape[1:3]
-    m = lax.broadcasted_iota(jnp.int32, (3 * GB, GB), 0) - GB
-    k = lax.broadcasted_iota(jnp.int32, (3 * GB, GB), 1)
-    apart = jnp.abs(m - k)
-    inside = (apart > guard[b]) & (apart <= guard[b] + train[b])
-    band = jnp.where(inside, 1.0, 0.0).astype(jnp.bfloat16)
-    band = jnp.concatenate([band, band], axis=0)
-    zeros = jnp.zeros((GB - EDGE, rows), jnp.float32)
-    after = jnp.concatenate([halo[0, 0], zeros], axis=0).T
-    before = jnp.concatenate([zeros, halo[0, 1]], axis=0).T
-    twice = 2.0 * train[b].astype(jnp.float32)
-    base = floor[b] * twice
-    cells = [before] + [power[0, j] for j in range(tiles)] + [after]
-    cells = [(x, *parts(x)) for x in cells]
-    for j in range(tiles):
-        near = cells[j:j + 3]
-        total = dot(jnp.concatenate([x[1] for x in near] + [x[2] for x in near], axis=1), band)
-        out[0, 0, :, j * GB:(j + 1) * GB] = near[1][0] * twice / (base + total)
+
+
+def write_kernel(ratio, out, sem):
+    beams, tiles = ratio.shape[:2]
+    copies = [
+        pltpu.make_async_copy(ratio.at[b, j], out.at[0, b, :, pl.ds(j * GB, GB)], sem.at[b, j])
+        for b in range(beams)
+        for j in range(tiles)
+    ]
+    for copy in copies:
+        copy.start()
+    for copy in copies:
+        copy.wait()
 
 
 def solution(mesh):
@@ -313,20 +363,19 @@
         ga = gates // GB
         tiles = ga // n
         groups = local // ROWS
+        half = pulses // 2
         consts = tables(gates, pulses)
+        first, second, third, last, twiddle, doppler = consts
         vmem = pl.BlockSpec(memory_space=pltpu.VMEM)
-        smem = pl.BlockSpec(memory_space=pltpu.SMEM)
         hbm = pl.BlockSpec(memory_space=pltpu.HBM)
-        f32, bf16 = jnp.float32, jnp.bfloat16
+        f32, bf16, i32 = jnp.float32, jnp.bfloat16, jnp.int32
         dma = pltpu.SemaphoreType.DMA
-        power, halo = pl.pallas_call(
+        room = 65472 * 1024 - 4 * beams * tiles * pulses * GB - 16 * 1024
+        ratio = pl.pallas_call(
             functools.partial(kernel, n, beams, pulses, gates),
-            out_shape=(
-                jax.ShapeDtypeStruct((beams, tiles, pulses, GB), f32),
-                jax.ShapeDtypeStruct((beams, 2, EDGE, pulses), f32),
-            ),
-            in_specs=[hbm, vmem, smem, vmem, vmem, vmem, vmem, vmem, hbm],
-            out_specs=(hbm, hbm),
+            out_shape=pltpu.VMEM((beams, tiles, pulses, GB), f32),
+            in_specs=[hbm] * 12,
+            out_specs=vmem,
             scratch_shapes=[
                 pltpu.VMEM((beams, groups, 2, ROWS, gates), f32),
                 pltpu.VMEM((2, ga * ROWS, GB), f32),
@@ -334,39 +383,47 @@
                 pltpu.VMEM((2, ga, GB), f32),
                 pltpu.VMEM((beams, 2, groups, ga, ROWS, GB), f32),
                 pltpu.VMEM((beams, 2, tiles, pulses // ROWS, ROWS, GB), f32),
-                pltpu.VMEM((2, 2, pulses, pulses // 2), bf16),
-                pltpu.VMEM((2, 3 * pulses // 2, 2 * GB), bf16),
-                pltpu.VMEM((2, pulses, 2 * GB), f32),
-                pltpu.VMEM((beams, tiles, pulses, GB), f32),
+                pltpu.VMEM((2, 2, pulses, half), bf16),
+                pltpu.VMEM((2, 3 * half, 2 * GB), bf16),
+                pltpu.VMEM((beams, tiles, 2, half, GB), f32),
+                pltpu.VMEM((beams, tiles, 2, half, GB), f32),
+                pltpu.VMEM((beams, tiles + 2, 2, half, GB), f32),
                 pltpu.VMEM((beams, 2, EDGE, pulses), f32),
                 pltpu.VMEM((beams, 2, EDGE, pulses), f32),
-                pltpu.VMEM((beams, 2, EDGE, pulses), f32),
+                pltpu.VMEM((beams, 2 * GB, 2 * GB), bf16),
+                pltpu.VMEM((2, gates), f32),
+                pltpu.SMEM((pulses,), f32),
+                pltpu.SMEM((beams,), i32),
+                pltpu.SMEM((beams,), i32),
+                pltpu.SMEM((beams,), f32),
+                pltpu.VMEM(first.shape, bf16),
+                pltpu.VMEM(second.shape, bf16),
+                pltpu.VMEM(third.shape, bf16),
+                pltpu.VMEM(last.shape, bf16),
+                pltpu.VMEM(twiddle.shape, f32),
                 dma((beams, groups)),
+                dma((10,)),
                 dma,
                 dma((beams,)),
                 dma((beams, tiles)),
                 dma((beams, 2)),
                 dma((beams, 2)),
-                dma((beams, tiles)),
-                dma((beams,)),
             ],
             compiler_params=pltpu.CompilerParams(
-                collective_id=0, has_side_effects=True, vmem_limit_bytes=60000 * 1024
+                collective_id=0, has_side_effects=True, vmem_limit_bytes=room
             ),
-        )(echoes, waveform, doppler_taper, *(jnp.asarray(c) for c in consts))
-        cut = pulses // 2
+        )(
+            echoes, waveform, doppler_taper, cfar_guard, cfar_train, noise_floor,
+            *(jnp.asarray(c) for c in consts),
+        )
         return pl.pallas_call(
-            cfar_kernel,
-            grid=(beams, pulses // cut),
-            out_shape=jax.ShapeDtypeStruct((1, beams, pulses, gates // n), f32),
-            in_specs=[
-                smem, smem, smem,
-                pl.BlockSpec((1, tiles, cut, GB), lambda b, q: (b, 0, q, 0)),
-                pl.BlockSpec((1, 2, EDGE, cut), lambda b, q: (b, 0, 0, q)),
-            ],
-            out_specs=pl.BlockSpec((1, 1, cut, tiles * GB), lambda b, q: (0, b, q, 0)),
-            compiler_params=pltpu.CompilerParams(vmem_limit_bytes=60000 * 1024),
-        )(cfar_guard, cfar_train, noise_floor, power, halo)
+            write_kernel,
+            out_shape=jax.ShapeDtypeStruct((1, beams, pulses, tiles * GB), f32),
+            in_specs=[vmem],
+            out_specs=hbm,
+            scratch_shapes=[dma((beams, tiles))],
+            compiler_params=pltpu.CompilerParams(vmem_limit_bytes=1024 * 1024),
+        )(ratio)
 
     in_specs = (
         P(None, None, "groups", "shard", None),

time: 105 us -> 101 us (0.962)
  Pallas kernels: 104 us -> 99.7 us
    pallas_call x1, Pallas kernels: 5.1 us -> 1.38 us  [step(): pl.pallas_call(write_kernel, out_shape=jax.ShapeDtypeStruct((1, beams, pu...]
where the time goes in v1:
time: 101 us; the launch traced here: 99.7 us
  Pallas kernels  99.7 us (99%)
    pallas_call x1, Pallas kernels, step(): pl.pallas_call(functools.partial(kernel, n, beams, pulses, gates), out_sh...  98.3 us

profile of v1, /device:TPU:9, one launch (start us, length us, event | category | flops | bytes accessed | tf_op | source)
XLA Modules:
  0.0 99.7 jit_solution(4745069586730718470)
XLA Ops:
  0.0 98.3 %shard_map.118.ratio = f32[2,4,512,128]{3,2,1,0:T(8,128)S(1)} custom-call(f32[1,2,2,32,8192]{4,3,2,1,0:T(8,128)} %echoes.1, f32[2,8192]{1,0:T(2,128)} %waveform_hbm.1, f32[512]{0:T(512)} %taper_hbm.1, s32[2]{0:T(128)} %guard_hbm.1, s32[2]{0:T(128)} %train_hbm.1, f32[2]{0:T(128)} %floor_hbm.1, bf16[256,256]{1,0:T(8,128)(2,1)} %constant.12.clone.first_hbm, ...), custom_call_target="tpu_custom_call" | custom-call | tf_op jit(solution)/shard_map/pallas_call | solution.py:374
  98.3 1.4 %shard_map.119 = f32[1,2,512,512]{3,2,1,0:T(8,128)} custom-call(f32[2,4,512,128]{3,2,1,0:T(8,128)S(1)} %shard_map.118.ratio), custom_call_target="tpu_custom_call" | custom-call | tf_op jit(solution)/shard_map/pallas_call | solution.py:419

commit v2 on v1

--- a/solution.py
+++ b/solution.py
@@ -29,8 +29,14 @@
     return np.cos(angles), np.sin(angles)
 
 
-def tables(gates, pulses):
+def slots(tiles):
+    return [0, tiles - 1, *range(tiles - 2, 0, -1)][:tiles]
+
+
+def tables(gates, pulses, n):
     ga = gates // GB
+    tiles = ga // n
+    rows = (np.arange(0, ga, tiles)[:, None] + np.array(slots(tiles))[None, :]).reshape(-1)
     ca, sa = dft(ga)
     cb, sb = dft(GB)
 
@@ -39,7 +45,7 @@
         return np.block([[high, high], [low, np.zeros_like(low)]])
 
     first = left(np.block([[ca, sa], [-sa, ca]]))
-    last = left(np.block([[ca, -sa], [sa, ca]]))
+    last = left(np.block([[ca[rows], -sa[rows]], [sa[rows], ca[rows]]]))
     per = GB // ga
     c = np.arange(GB).reshape(GB // per, per).T.reshape(-1)
     cb, sb = cb[:, c], sb[:, c]
@@ -79,13 +85,18 @@
     tiles = ga // n
     groups = pulses // n // ROWS
     half = pulses // 2
-    order = sorted(range(1, n), key=lambda k: (abs(2 * k - n), k))
+    place = slots(tiles)
+    outer = min(2, tiles)
+    side = n // 2
+    mine = lax.rem(me, side)
+    far, here = side - (me - mine), me - mine
+    across = [far + k for k in range(side)]
+    near = [here + lax.rem(mine + k, side) for k in range(1, side)]
+    order = across[:1] + [to for pair in zip(near, across[1:]) for to in pair]
 
     barrier = pltpu.get_barrier_semaphore()
-    for k in order:
-        pl.semaphore_signal(
-            barrier, inc=1, device_id={"shard": lax.rem(me + k, n)}, device_id_type=MESH
-        )
+    for to in order:
+        pl.semaphore_signal(barrier, inc=1, device_id={"shard": to}, device_id_type=MESH)
 
     def load(b, pg):
         start = pg * ROWS if isinstance(pg, int) else pl.multiple_of(pg * ROWS, ROWS)
@@ -108,11 +119,6 @@
     load(0, 0).start()
     for copy in small[1:]:
         copy.start()
-    for b in range(beams):
-        for pg in range(groups):
-            if b or pg:
-                load(b, pg).start()
-    table_copy.start()
 
     per = GB // ga
     scale = 1.0 / (gates * math.sqrt(pulses))
@@ -125,12 +131,24 @@
         filt[c] = jnp.concatenate(turned, axis=0).T[:ga]
     for copy in small[1:]:
         copy.wait()
+    load(0, 0).wait()
+    for b in range(beams):
+        for pg in range(groups):
+            if b or pg:
+                load(b, pg).start()
+    table_copy.start()
 
     def stacked(ref):
         return jnp.concatenate([ref[0], ref[0], ref[1]], axis=0)
 
     def compress(b, pg):
-        load(b, pg).wait()
+        if b:
+            load(b, pg).wait()
+        else:
+            @pl.when(pg > 0)
+            def _():
+                load(b, pg).wait()
+
         for c in range(2):
             for i in range(ga):
                 xs[c, i * ROWS:(i + 1) * ROWS, :] = xin[b, pg, c, :, i * GB:(i + 1) * GB]
@@ -176,38 +194,34 @@
                         c * ga:(c + 1) * ga, e * GB:(e + 1) * GB
                     ]
 
-    def send_group(b, pg):
-        dst = got.at[b, :, :, me * groups + pg]
-        for k in order:
-            to = lax.rem(me + k, n)
+    def send(src, dst, b, sem, peers, keep):
+        for to in peers:
             pltpu.make_async_remote_copy(
-                src_ref=sent.at[b, :, pg, pl.ds(to * tiles, tiles)],
+                src_ref=src(to),
                 dst_ref=dst,
                 send_sem=send_sem.at[b],
-                recv_sem=recv_sem.at[b, 0],
+                recv_sem=recv_sem.at[b, sem],
                 device_id={"shard": to},
                 device_id_type=MESH,
             ).start()
-        pltpu.make_async_copy(
-            sent.at[b, :, pg, pl.ds(me * tiles, tiles)], dst, recv_sem.at[b, 0]
-        ).start()
-
-    def send_tile(b, j):
-        dst = got.at[b, :, j, pl.ds(me * groups, groups)]
-        for k in order:
-            to = lax.rem(me + k, n)
-            pltpu.make_async_remote_copy(
-                src_ref=sent.at[b, :, :, to * tiles + j],
-                dst_ref=dst,
-                send_sem=send_sem.at[b],
-                recv_sem=recv_sem.at[b, j],
-                device_id={"shard": to},
-                device_id_type=MESH,
-            ).start()
-        pltpu.make_async_copy(sent.at[b, :, :, me * tiles + j], dst, recv_sem.at[b, j]).start()
+        if keep:
+            pltpu.make_async_copy(src(me), dst, recv_sem.at[b, sem]).start()
+
+    def send_group(b, pg):
+        send(
+            lambda to: sent.at[b, :, pg, pl.ds(to * tiles, outer)],
+            got.at[b, :, pl.ds(0, outer), me * groups + pg],
+            b, 0, order, True,
+        )
+
+    def send_slot(b, t, peers, keep):
+        send(
+            lambda to: sent.at[b, :, :, to * tiles + t],
+            got.at[b, :, t, pl.ds(me * groups, groups)],
+            b, t, peers, keep,
+        )
 
     for b in range(beams):
-        final = b == beams - 1
 
         @pl.loop(0, groups)
         def _(pg):
@@ -217,13 +231,11 @@
                 def _():
                     pl.semaphore_wait(barrier, n - 1)
 
-            if not final:
-                send_group(b, pg)
-
-        if final:
-            @pl.loop(0, tiles)
-            def _(t):
-                send_tile(b, lax.rem(t * (tiles - 1), tiles))
+            send_group(b, pg)
+
+    for t in range(outer, tiles - 1):
+        for b in range(beams):
+            send_slot(b, t, order, True)
 
     table_copy.wait()
 
@@ -239,8 +251,9 @@
     def sums(b, x):
         return dot(jnp.concatenate(parts(x), axis=1), band[b])
 
-    def transform(b, j, then=None):
-        x = jnp.concatenate([got[b, c, j].reshape(pulses, GB) for c in range(2)], axis=1)
+    def transform(b, t, then=None):
+        j = place[t]
+        x = jnp.concatenate([got[b, c, t].reshape(pulses, GB) for c in range(2)], axis=1)
         for e, y in enumerate((x[:half] + x[half:], x[:half] - x[half:])):
             high, low = parts(y)
             rhs[e, 0:half] = high
@@ -298,43 +311,47 @@
             cross[b, 0, e] = total
             cross[b, tiles + 1, e] = total
 
-    for b in range(beams - 1):
-        pltpu.make_async_copy(got.at[b], got.at[b], recv_sem.at[b, 0]).wait()
-
-        @pl.loop(0, tiles)
-        def _(j):
-            transform(b, j)
-
+    for b in range(beams):
+        arrived = got.at[b, :, pl.ds(0, outer)]
+        pltpu.make_async_copy(arrived, arrived, recv_sem.at[b, 0]).wait()
+        for t in range(outer):
+            transform(b, t)
         send_edges(b)
 
-    b = beams - 1
-    done = set()
-    ready = set()
-
-    def ratios(e):
+    if tiles > outer:
+        for b in range(beams):
+            send_slot(b, tiles - 1, near, True)
+        for b in range(beams):
+            send_slot(b, tiles - 1, across, False)
+
+    done = [set() for _ in range(beams)]
+
+    def ratios(b, ready, e):
         for j in range(tiles):
-            if j not in done and {j - 1, j, j + 1} & set(range(tiles)) <= ready:
+            if j not in done[b] and {j - 1, j, j + 1} & set(range(tiles)) <= ready:
                 ratio(b, j, e)
                 if e == 1:
-                    done.add(j)
-
-    for t in range(tiles):
-        j = t * (tiles - 1) % tiles
-        arrived = got.at[b, :, j]
-        pltpu.make_async_copy(arrived, arrived, recv_sem.at[b, j]).wait()
-        ready.add(j)
-        transform(b, j, ratios if 2 < tiles == t + 1 else None)
-        if t == min(1, tiles - 1):
-            send_edges(b)
-        if t == max(tiles - 2, min(1, tiles - 1)):
-            for i in range(beams):
-                take_edges(i)
-            for i in range(beams - 1):
-                for jj in range(tiles):
-                    for e in range(2):
-                        ratio(i, jj, e)
+                    done[b].add(j)
+
+    for t in range(outer, tiles):
+        ready = set(place[:t + 1])
+        for b in range(beams):
+            arrived = got.at[b, :, t]
+            pltpu.make_async_copy(arrived, arrived, recv_sem.at[b, t]).wait()
+            final = t == tiles - 1
+            transform(b, t, functools.partial(ratios, b, ready) if final and t > outer else None)
+        if t == max(outer, tiles - 2):
+            for b in range(beams):
+                take_edges(b)
+        if not final or t == outer:
+            for b in range(beams):
+                for e in range(2):
+                    ratios(b, ready, e)
+    if tiles == outer:
+        for b in range(beams):
+            take_edges(b)
             for e in range(2):
-                ratios(e)
+                ratios(b, set(range(tiles)), e)
 
     for b in range(beams):
         whole = sent.at[b, :, :, pl.ds(0, (n - 1) * tiles)]
@@ -364,7 +381,7 @@
         tiles = ga // n
         groups = local // ROWS
         half = pulses // 2
-        consts = tables(gates, pulses)
+        consts = tables(gates, pulses, n)
         first, second, third, last, twiddle, doppler = consts
         vmem = pl.BlockSpec(memory_space=pltpu.VMEM)
         hbm = pl.BlockSpec(memory_space=pltpu.HBM)

time: 101 us -> 99.4 us (0.984); the launches traced: 99.7 us -> 99.3 us
  no operation moved by 1% of the time
where the time goes in v2:
time: 99.4 us; the launch traced here: 99.3 us
  Pallas kernels  99.3 us (100%)
    pallas_call x1, Pallas kernels, step(): pl.pallas_call(functools.partial(kernel, n, beams, pulses, gates), out_sh...  97.9 us

profile of v2, /device:TPU:9, one launch (start us, length us, event | category | flops | bytes accessed | tf_op | source)
XLA Modules:
  0.0 99.3 jit_solution(18190965930412502773)
XLA Ops:
  0.0 97.9 %shard_map.118.ratio = f32[2,4,512,128]{3,2,1,0:T(8,128)S(1)} custom-call(f32[1,2,2,32,8192]{4,3,2,1,0:T(8,128)} %echoes.1, f32[2,8192]{1,0:T(2,128)} %waveform_hbm.1, f32[512]{0:T(512)} %taper_hbm.1, s32[2]{0:T(128)} %guard_hbm.1, s32[2]{0:T(128)} %train_hbm.1, f32[2]{0:T(128)} %floor_hbm.1, bf16[256,256]{1,0:T(8,128)(2,1)} %constant.12.clone.first_hbm, ...), custom_call_target="tpu_custom_call" | custom-call | tf_op jit(solution)/shard_map/pallas_call | solution.py:391
  97.9 1.4 %shard_map.119 = f32[1,2,512,512]{3,2,1,0:T(8,128)} custom-call(f32[2,4,512,128]{3,2,1,0:T(8,128)S(1)} %shard_map.118.ratio), custom_call_target="tpu_custom_call" | custom-call | tf_op jit(solution)/shard_map/pallas_call | solution.py:436

commit v3 on v2

v3 whole, which is shorter than its diff:
```python
import functools
import math

import jax
import jax.numpy as jnp
import numpy as np
from jax import lax
from jax.experimental import pallas as pl
from jax.experimental.pallas import tpu as pltpu
from jax.sharding import PartitionSpec as P

GB = 128
ROWS = 8
EDGE = 20
MESH = pl.DeviceIdType.MESH


def split(table):
    table = np.asarray(table, np.float32)
    high = table.astype(jnp.bfloat16)
    low = (table - high.astype(np.float32)).astype(jnp.bfloat16)
    return high, low


def dft(length, size=None):
    size = size or length
    i = np.arange(size)[:, None] * np.arange(length)[None, :] % length
    angles = 2.0 * np.pi / length * i
    return np.cos(angles), np.sin(angles)


def slots(tiles):
    return [0, tiles - 1, *range(tiles - 2, 0, -1)][:tiles]


def waiting(tiles):
    if tiles <= 2:
        return []
    j = slots(tiles)[-1]
    return [j, j - 1, j + 1]


def tables(gates, pulses, n):
    ga = gates // GB
    tiles = ga // n
    rows = (np.arange(0, ga, tiles)[:, None] + np.array(slots(tiles))[None, :]).reshape(-1)
    ca, sa = dft(ga)
    cb, sb = dft(GB)

    def left(matrix):
        high, low = split(matrix)
        return np.block([[high, high], [low, np.zeros_like(low)]])

    first = left(np.block([[ca, sa], [-sa, ca]]))
    last = left(np.block([[ca[rows], -sa[rows]], [sa[rows], ca[rows]]]))
    per = GB // ga
    c = np.arange(GB).reshape(GB // per, per).T.reshape(-1)
    cb, sb = cb[:, c], sb[:, c]
    second = np.stack(split(np.block([[cb, -sb], [sb, cb]])))
    third = np.stack(split(np.block([[cb.T, sb.T], [-sb.T, cb.T]])))
    i = np.arange(ga)[:, None] * np.arange(GB)[None, :] % gates
    twiddle = np.stack([np.cos(2 * np.pi / gates * i), np.sin(2 * np.pi / gates * i)])
    half = pulses // 2
    cp, sp = dft(pulses)
    doppler = [
        np.stack(split(np.concatenate([cp[e::2, :half], sp[e::2, :half]], axis=0))) for e in range(2)
    ]
    return np.stack([first, *second, *third, last]), twiddle.astype(np.float32), np.stack(doppler)


def parts(x):
    high = x.astype(jnp.bfloat16)
    low = (x - high.astype(jnp.float32)).astype(jnp.bfloat16)
    return high, low


def dot(a, b):
    return jnp.dot(a, b, preferred_element_type=jnp.float32)


def kernel(
    n, beams, pulses, gates,
    echoes, waveform_hbm, taper_hbm, guard_hbm, train_hbm, floor_hbm,
    chain_hbm, twiddle_hbm, doppler_hbm,
    out, num, den, over,
    xin, xs, wave, filt, sent, got, table, rhs, power, own, cross, edge, halo, band,
    waveform, taper, guard, train, floor, chain, twiddle,
    in_sem, small_sem, send_sem, recv_sem, edge_send, edge_recv,
):
    me = lax.axis_index("shard")
    ga = gates // GB
    tiles = ga // n
    groups = pulses // n // ROWS
    half = pulses // 2
    place = slots(tiles)
    outer = min(2, tiles)
    side = n // 2
    mine = lax.rem(me, side)
    far, here = side - (me - mine), me - mine
    across = [far + lax.rem(k + far // 2, side) for k in range(side)]
    near = [here + lax.rem(mine + k, side) for k in range(1, side)]
    order = across[:1] + [to for pair in zip(near, across[1:]) for to in pair]

    barrier = pltpu.get_barrier_semaphore()
    for to in order:
        pl.semaphore_signal(barrier, inc=1, device_id={"shard": to}, device_id_type=MESH)

    def load(b, start, size, sem):
        return pltpu.make_async_copy(
            echoes.at[0, :, b, pl.ds(start, size), :], xin.at[b, :, pl.ds(start, size)], in_sem.at[sem]
        )

    local = groups * ROWS
    loads = [load(0, 0, ROWS, beams)]
    loads += [load(0, ROWS, local - ROWS, 0)] if groups > 1 else []
    loads += [load(b, 0, local, b) for b in range(1, beams)]
    small = [
        pltpu.make_async_copy(src, dst, small_sem.at[i])
        for i, (src, dst) in enumerate(
            ((waveform_hbm, waveform), (chain_hbm, chain), (twiddle_hbm, twiddle), (taper_hbm, taper))
        )
    ]
    later = [
        pltpu.make_async_copy(src, dst, small_sem.at[i])
        for i, (src, dst) in enumerate(
            ((doppler_hbm, table), (guard_hbm, guard), (train_hbm, train), (floor_hbm, floor))
        )
    ]
    small[0].start()
    loads[0].start()
    for copy in small[1:]:
        copy.start()

    per = GB // ga
    scale = 1.0 / (gates * math.sqrt(pulses))
    small[0].wait()
    for c in range(2):
        for m in range(ga):
            wave[m:m + 1, :] = waveform[c:c + 1, m * GB:(m + 1) * GB]
        lines = wave[...] * scale
        turned = [lines] + [pltpu.roll(lines, GB - h * ga, axis=1) for h in range(1, per)]
        filt[c] = jnp.concatenate(turned, axis=0).T[:ga]
    def stage(i):
        return jnp.concatenate([chain[i], chain[i], chain[i + 1]], axis=0)

    def compress(b, pg):
        row = pg * ROWS if isinstance(pg, int) else pl.multiple_of(pg * ROWS, ROWS)
        for c in range(2):
            for i in range(ga):
                xs[c, i * ROWS:(i + 1) * ROWS, :] = xin[b, c, pl.ds(row, ROWS), i * GB:(i + 1) * GB]
        tc, ts = twiddle[0], twiddle[1]
        lhs = []
        for p in range(0, ROWS, 2):
            x = jnp.concatenate(
                [
                    jnp.concatenate([xs[c, pl.ds(p + e, ga, stride=ROWS), :] for c in range(2)], axis=0)
                    for e in range(2)
                ],
                axis=1,
            )
            y = dot(chain[0], jnp.concatenate(parts(x), axis=0))
            y = y[:2 * ga] + y[2 * ga:]
            for e in range(2):
                yr, yi = y[:ga, e * GB:(e + 1) * GB], y[ga:, e * GB:(e + 1) * GB]
                z = jnp.concatenate([yr * tc + yi * ts, yi * tc - yr * ts], axis=1)
                high, low = parts(z)
                lhs.append(jnp.concatenate([high, low, high], axis=1))
        x = dot(jnp.concatenate(lhs, axis=0), stage(1))
        lhs = []
        fr, fi = filt[0], filt[1]
        for p in range(ROWS):
            weight = taper[(me * groups + pg) * ROWS + p]
            hr, hi = fr * weight, fi * weight
            xr, xi = x[p * ga:(p + 1) * ga, :GB], x[p * ga:(p + 1) * ga, GB:]
            z = jnp.concatenate([xr * hr + xi * hi, xi * hr - xr * hi], axis=1)
            high, low = parts(z)
            lhs.append(jnp.concatenate([high, low, high], axis=1))
        x = dot(jnp.concatenate(lhs, axis=0), stage(3))
        for p in range(0, ROWS, 2):
            pair = []
            for e in range(2):
                r = (p + e) * ga
                xr, xi = x[r:r + ga, :GB], x[r:r + ga, GB:]
                pair.append(jnp.concatenate([xr * tc - xi * ts, xi * tc + xr * ts], axis=0))
            y = dot(chain[5], jnp.concatenate(parts(jnp.concatenate(pair, axis=1)), axis=0))
            y = y[:2 * ga] + y[2 * ga:]
            for e in range(2):
                for c in range(2):
                    sent.at[b, c, pg].reshape(ga * ROWS, GB)[pl.ds(p + e, ga, stride=ROWS), :] = y[
                        c * ga:(c + 1) * ga, e * GB:(e + 1) * GB
                    ]

    def send(src, dst, sem, peers, keep):
        for to in peers:
            pltpu.make_async_remote_copy(
                src_ref=src(to),
                dst_ref=dst,
                send_sem=send_sem,
                recv_sem=sem,
                device_id={"shard": to},
                device_id_type=MESH,
            ).start()
        if keep:
            pltpu.make_async_copy(src(me), dst, sem).start()

    def send_groups(b, pg, count):
        send(
            lambda to: sent.at[b, :, pl.ds(pg, count), pl.ds(to * tiles, outer)],
            got.at[b, :, pl.ds(me * groups + pg, count), pl.ds(0, outer)],
            recv_sem.at[b, 0], order, True,
        )

    def send_slot(b, t, peers, keep):
        send(
            lambda to: sent.at[b, :, :, to * tiles + t],
            got.at[b, :, pl.ds(me * groups, groups), t],
            recv_sem.at[b, t - outer + 1], peers, keep,
        )

    for copy in small[1:]:
        copy.wait()
    loads[0].wait()
    for copy in loads[1:2]:
        copy.start()
    compress(0, 0)
    pl.semaphore_wait(barrier, n - 1)
    send_groups(0, 0, 1)
    for copy in loads[2:] + later:
        copy.start()
    for b in range(beams):
        begin = 1 if b == 0 else 0
        if begin < groups:
            loads[b + 1 if groups > 1 else b].wait()

        @pl.loop(begin, groups)
        def _(pg):
            compress(b, pg)

            @pl.when(lax.rem(pg - begin, 2) == 1)
            def _():
                send_groups(b, pg - 1, 2)

            if (groups - begin) % 2:
                @pl.when(pg == groups - 1)
                def _():
                    send_groups(b, pg, 1)

    for t in range(outer, tiles - 1):
        for b in range(beams):
            send_slot(b, t, order, True)

    for copy in later:
        copy.wait()

    m = lax.broadcasted_iota(jnp.int32, (GB, 2 * GB), 0)
    k = lax.broadcasted_iota(jnp.int32, (GB, 2 * GB), 1)
    apart = jnp.where(k < GB, jnp.abs(m - k), jnp.where(k < GB + GB // 2, k - m, m + 2 * GB - k))
    for b in range(beams):
        inside = (apart > guard[b]) & (apart <= guard[b] + train[b])
        lines = jnp.where(inside, 1.0, 0.0).astype(jnp.bfloat16)
        band[b, :GB] = lines
        band[b, GB:] = lines

    def sums(b, x):
        return dot(jnp.concatenate(parts(x), axis=1), band[b])

    pending = waiting(tiles)

    def transform(b, t, final=False):
        j = place[t]
        x = jnp.concatenate([got[b, c, :, t].reshape(pulses, GB) for c in range(2)], axis=1)
        for e, y in enumerate((x[:half] + x[half:], x[:half] - x[half:])):
            high, low = parts(y)
            rhs[e, 0:half] = high
            rhs[e, half:2 * half] = low
            rhs[e, 2 * half:] = high
        for e in range(2):
            lhs = jnp.concatenate([table[e, 0], table[e, 0], table[e, 1]], axis=1)
            spec = dot(lhs, rhs[e])
            re = spec[:half, :GB] + spec[half:, GB:]
            im = spec[:half, GB:] - spec[half:, :GB]
            p = re * re + im * im
            power[b, j, e] = p
            total = sums(b, p)
            own[b, j, e] = total[:, :GB]
            cross[b, j + 1, e] = total[:, GB:]
            if final:
                over[e] = total[:, GB:]
                num[0, e] = p * scaled(b)
                den[0, e] = total[:, :GB] + den[0, e]

    def scaled(b):
        return 2.0 * train[b].astype(jnp.float32)

    def lower():
        return lax.broadcasted_iota(jnp.int32, (half, GB), 1) < GB // 2

    def ratio(b, j, e):
        total = own[b, j, e] + jnp.where(lower(), cross[b, j, e], cross[b, j + 2, e])
        out.at[b, j][pl.ds(e, half, stride=2), :] = (
            power[b, j, e] * scaled(b) / (floor[b] * scaled(b) + total)
        )

    def prepare(b, e):
        base = floor[b] * scaled(b)
        den[0, e] = jnp.where(lower(), cross[b, pending[0], e], cross[b, pending[0] + 2, e]) + base
        for i, j in enumerate(pending[1:], 1):
            num[i, e] = power[b, j, e] * scaled(b)
            part = jnp.where(lower(), cross[b, j, e], 0.0) if j < pending[0] else jnp.where(lower(), 0.0, cross[b, j + 2, e])
            den[i, e] = own[b, j, e] + part + base

    def send_edges(b):
        for side in range(2):
            cut = slice(0, EDGE) if side == 0 else slice(GB - EDGE, GB)
            for e in range(2):
                x = power[b, (tiles - 1) * side, e].T[cut]
                for i in range(half // GB):
                    start = (e * (half // GB) + i) * EDGE
                    edge[b, side, start:start + EDGE] = x[:, i * GB:(i + 1) * GB]
            pltpu.make_async_remote_copy(
                src_ref=edge.at[b, side],
                dst_ref=halo.at[b, side],
                send_sem=edge_send,
                recv_sem=edge_recv,
                device_id={"shard": lax.rem(me + (n - 1 if side == 0 else 1), n)},
                device_id_type=MESH,
            ).start()

    def take_edges():
        pltpu.make_async_copy(edge, edge, edge_send).wait()
        pltpu.make_async_copy(halo, halo, edge_recv).wait()
        zeros = jnp.zeros((GB - 2 * EDGE, half), jnp.float32)

        def lines(b, side, e):
            start = [(e * (half // GB) + i) * EDGE for i in range(half // GB)]
            x = jnp.concatenate([halo[b, side, i:i + EDGE] for i in start], axis=1)
            return jnp.where(me > 0 if side else me < n - 1, x, 0.0)

        for b in range(beams):
            for e in range(2):
                x = jnp.concatenate([lines(b, 0, e), zeros, lines(b, 1, e)], axis=0).T
                total = sums(b, x)[:, GB:]
                cross[b, 0, e] = total
                cross[b, tiles + 1, e] = total

    for b in range(beams):
        arrived = got.at[b, :, :, pl.ds(0, outer)]
        pltpu.make_async_copy(arrived, arrived, recv_sem.at[b, 0]).wait()
        for t in range(outer):
            transform(b, t)
        send_edges(b)

    if tiles > outer:
        for b in range(beams):
            send_slot(b, tiles - 1, near, True)
        for b in range(beams):
            send_slot(b, tiles - 1, across, False)

    done = [set() for _ in range(beams)]

    def ratios(b, ready, e):
        for j in range(tiles):
            if b == beams - 1 and j in pending:
                continue
            if j not in done[b] and {j - 1, j, j + 1} & set(range(tiles)) <= ready:
                ratio(b, j, e)
                if e == 1:
                    done[b].add(j)

    for t in range(outer, tiles):
        ready = set(place[:t + 1])
        for b in range(beams):
            final = t == tiles - 1 and b == beams - 1
            if final:
                if t == outer:
                    take_edges()
                for e in range(2):
                    prepare(b, e)
            arrived = got.at[b, :, :, t]
            pltpu.make_async_copy(arrived, arrived, recv_sem.at[b, t - outer + 1]).wait()
            transform(b, t, final)
            if t == tiles - 1 and not final and t > outer:
                for e in range(2):
                    ratios(b, ready, e)
        if t == tiles - 2:
            take_edges()
            for b in range(beams):
                for e in range(2):
                    ratios(b, ready, e)
    if tiles == outer:
        take_edges()
    if tiles <= outer + 1:
        for b in range(beams):
            for e in range(2):
                ratios(b, set(place), e)

    whole = sent.at[:, :, :, pl.ds(0, (n - 1) * tiles)]
    pltpu.make_async_copy(whole, whole, send_sem).wait()


def write_kernel(ratio, num, den, over, out, late, sem):
    beams, tiles = ratio.shape[:2]
    pending = waiting(tiles)
    half = num.shape[2]

    def put(b, j):
        i = pending.index(j) if b == beams - 1 and j in pending else None
        src = ratio.at[b, j] if i is None else late.at[i]
        return pltpu.make_async_copy(src, out.at[0, b, :, pl.ds(j * GB, GB)], sem)

    for b in range(beams):
        for j in range(tiles):
            if b < beams - 1 or j not in pending:
                put(b, j).start()
    lower = lax.broadcasted_iota(jnp.int32, (half, GB), 1) < GB // 2
    for i, j in enumerate(pending):
        for e in range(2):
            total = den[i, e]
            if i:
                total += jnp.where(lower == (j > pending[0]), over[e], 0.0)
            late.at[i][pl.ds(e, half, stride=2), :] = num[i, e] / total
        put(beams - 1, j).start()
    pltpu.make_async_copy(ratio, ratio, sem).wait()


def solution(mesh):
    n = mesh.shape["shard"]

    def step(echoes, waveform, doppler_taper, cfar_guard, cfar_train, noise_floor):
        beams, local, gates = echoes.shape[2:]
        pulses = local * n
        ga = gates // GB
        tiles = ga // n
        groups = local // ROWS
        half = pulses // 2
        consts = tables(gates, pulses, n)
        chain, twiddle, _ = consts
        vmem = pl.BlockSpec(memory_space=pltpu.VMEM)
        hbm = pl.BlockSpec(memory_space=pltpu.HBM)
        f32, bf16, i32 = jnp.float32, jnp.bfloat16, jnp.int32
        dma = pltpu.SemaphoreType.DMA
        late = max(1, len(waiting(tiles)))
        held = (
            (beams, tiles, pulses, GB), (late, 2, half, GB), (late, 2, half, GB), (2, half, GB),
        )
        room = 65456 * 1024 - sum(4 * math.prod(shape) for shape in held)
        results = pl.pallas_call(
            functools.partial(kernel, n, beams, pulses, gates),
            out_shape=tuple(pltpu.VMEM(shape, f32) for shape in held),
            in_specs=[hbm] * 9,
            out_specs=(vmem,) * 4,
            scratch_shapes=[
                pltpu.VMEM((beams, 2, local, gates), f32),
                pltpu.VMEM((2, ga * ROWS, GB), f32),
                pltpu.VMEM((ga, GB), f32),
                pltpu.VMEM((2, ga, GB), f32),
                pltpu.VMEM((beams, 2, groups, ga, ROWS, GB), f32),
                pltpu.VMEM((beams, 2, pulses // ROWS, tiles, ROWS, GB), f32),
                pltpu.VMEM((2, 2, pulses, half), bf16),
                pltpu.VMEM((2, 3 * half, 2 * GB), bf16),
                pltpu.VMEM((beams, tiles, 2, half, GB), f32),
                pltpu.VMEM((beams, tiles, 2, half, GB), f32),
                pltpu.VMEM((beams, tiles + 2, 2, half, GB), f32),
                pltpu.VMEM((beams, 2, pulses // GB * EDGE, GB), f32),
                pltpu.VMEM((beams, 2, pulses // GB * EDGE, GB), f32),
                pltpu.VMEM((beams, 2 * GB, 2 * GB), bf16),
                pltpu.VMEM((2, gates), f32),
                pltpu.SMEM((pulses,), f32),
                pltpu.SMEM((beams,), i32),
                pltpu.SMEM((beams,), i32),
                pltpu.SMEM((beams,), f32),
                pltpu.VMEM(chain.shape, bf16),
                pltpu.VMEM(twiddle.shape, f32),
                dma((beams + 1,)),
                dma((4,)),
                dma,
                dma((beams, tiles - min(2, tiles) + 1)),
                dma,
                dma,
            ],
            compiler_params=pltpu.CompilerParams(
                collective_id=0, has_side_effects=True, vmem_limit_bytes=room
            ),
        )(
            echoes, waveform, doppler_taper, cfar_guard, cfar_train, noise_floor,
            *(jnp.asarray(c) for c in consts),
        )
        return pl.pallas_call(
            write_kernel,
            out_shape=jax.ShapeDtypeStruct((1, beams, pulses, tiles * GB), f32),
            in_specs=[vmem] * 4,
            out_specs=hbm,
            scratch_shapes=[pltpu.VMEM((late, pulses, GB), f32), dma],
            compiler_params=pltpu.CompilerParams(vmem_limit_bytes=2048 * 1024),
        )(*results)

    in_specs = (
        P(None, None, "groups", "shard", None),
        P(),
        P(),
        P("groups"),
        P("groups"),
        P("groups"),
    )
    return jax.shard_map(
        step, mesh=mesh, in_specs=in_specs, out_specs=P(None, "groups", None, "shard"), check_vma=False
    )
```

time: 99.4 us -> 99 us (level)
  no operation moved by 1% of the time
where the time goes in v3:
time: 99 us; the launch traced here: 98.9 us
  Pallas kernels  98.9 us (100%)
    pallas_call x1, Pallas kernels, step(): pl.pallas_call(functools.partial(kernel, n, beams, pulses, gates), out_sh...  97.6 us

profile of v3, /device:TPU:9, one launch (start us, length us, event | category | flops | bytes accessed | tf_op | source)
XLA Modules:
  0.0 98.9 jit_solution(7585921634984785634)
XLA Ops:
  0.0 97.6 %shard_map.91 = (f32[2,4,512,128]{3,2,1,0:T(8,128)S(1)}, f32[3,2,256,128]{3,2,1,0:T(8,128)S(1)}, f32[3,2,256,128]{3,2,1,0:T(8,128)S(1)}, f32[2,256,128]{2,1,0:T(8,128)S(1)}) custom-call(f32[1,2,2,32,8192]{4,3,2,1,0:T(8,128)} %echoes.1, f32[2,8192]{1,0:T(2,128)} %waveform_hbm.1, f32[512]{0:T(512)} %taper_hbm.1, s32[2]{0:T(128)} %guard_hbm.1, s32[2]{0:T(128)} %train_hbm.1, ...), custom_call_target="tpu_custom_call" | custom-call | tf_op jit(solution)/shard_map/pallas_call | solution.py:447
  97.6 1.3 %shard_map.92 = f32[1,2,512,512]{3,2,1,0:T(8,128)} custom-call(f32[2,4,512,128]{3,2,1,0:T(8,128)S(1)} %get-tuple-element.9.ratio, f32[3,2,256,128]{3,2,1,0:T(8,128)S(1)} %get-tuple-element.10.num, f32[3,2,256,128]{3,2,1,0:T(8,128)S(1)} %get-tuple-element.11.den, f32[2,256,128]{2,1,0:T(8,128)S(1)} %get-tuple-element.12.over), custom_call_target="tpu_custom_call" | custom-call | tf_op jit(solution)/shard_map/pallas_call | solution.py:488

commit v4 on v3

--- a/solution.py
+++ b/solution.py
@@ -12,6 +12,7 @@
 GB = 128
 ROWS = 8
 EDGE = 20
+RADIX = 4
 MESH = pl.DeviceIdType.MESH
 
 
@@ -60,10 +61,11 @@
     third = np.stack(split(np.block([[cb.T, sb.T], [-sb.T, cb.T]])))
     i = np.arange(ga)[:, None] * np.arange(GB)[None, :] % gates
     twiddle = np.stack([np.cos(2 * np.pi / gates * i), np.sin(2 * np.pi / gates * i)])
-    half = pulses // 2
+    part = pulses // RADIX
     cp, sp = dft(pulses)
     doppler = [
-        np.stack(split(np.concatenate([cp[e::2, :half], sp[e::2, :half]], axis=0))) for e in range(2)
+        np.stack(split(np.concatenate([cp[e::RADIX, :part], sp[e::RADIX, :part]], axis=0)))
+        for e in range(RADIX)
     ]
     return np.stack([first, *second, *third, last]), twiddle.astype(np.float32), np.stack(doppler)
 
@@ -78,12 +80,37 @@
     return jnp.dot(a, b, preferred_element_type=jnp.float32)
 
 
+def rotated(x):
+    if len(x) == 2:
+        return [[p + q for p, q in zip(*x)], [p - q for p, q in zip(*x)]]
+    (ar, ai), (br, bi), (cr, ci), (dr, di) = x
+    sr, si, tr, ti = ar + cr, ai + ci, ar - cr, ai - ci
+    ur, ui, vr, vi = br + dr, bi + di, br - dr, bi - di
+    return [(sr + ur, si + ui), (tr + vi, ti - vr), (sr - ur, si - ui), (tr - vi, ti + vr)]
+
+
+def stacked(high, low, axis):
+    return jnp.concatenate([high, high, low] if axis else [high, low, high], axis=axis)
+
+
+def intensity(table, high, low):
+    spec = dot(stacked(table[0], table[1], 1), stacked(high, low, 0))
+    part = spec.shape[0] // 2
+    re = spec[:part, :GB] + spec[part:, GB:]
+    im = spec[:part, GB:] - spec[part:, :GB]
+    return re * re + im * im
+
+
+def sums(x, band):
+    return dot(jnp.concatenate(parts(x), axis=1), band)
+
+
 def kernel(
     n, beams, pulses, gates,
     echoes, waveform_hbm, taper_hbm, guard_hbm, train_hbm, floor_hbm,
     chain_hbm, twiddle_hbm, doppler_hbm,
-    out, num, den, over,
-    xin, xs, wave, filt, sent, got, table, rhs, power, own, cross, edge, halo, band,
+    out, num, den, tail, table, sieve, factor,
+    xin, xs, wave, filt, sent, got, rhs, power, own, cross, edge, halo, band,
     waveform, taper, guard, train, floor, chain, twiddle,
     in_sem, small_sem, send_sem, recv_sem, edge_send, edge_recv,
 ):
@@ -91,13 +118,13 @@
     ga = gates // GB
     tiles = ga // n
     groups = pulses // n // ROWS
-    half = pulses // 2
+    part = pulses // RADIX
     place = slots(tiles)
     outer = min(2, tiles)
     side = n // 2
     mine = lax.rem(me, side)
     far, here = side - (me - mine), me - mine
-    across = [far + lax.rem(k + far // 2, side) for k in range(side)]
+    across = [far + k for k in range(side)]
     near = [here + lax.rem(mine + k, side) for k in range(1, side)]
     order = across[:1] + [to for pair in zip(near, across[1:]) for to in pair]
 
@@ -261,43 +288,33 @@
         band[b, :GB] = lines
         band[b, GB:] = lines
 
-    def sums(b, x):
-        return dot(jnp.concatenate(parts(x), axis=1), band[b])
-
     pending = waiting(tiles)
 
-    def transform(b, t, final=False):
+    def branches(b, t):
+        x = [got[b, c, :, t].reshape(RADIX, part, GB) for c in range(2)]
+        return [parts(jnp.concatenate(y, axis=1)) for y in rotated([(x[0][i], x[1][i]) for i in range(RADIX)])]
+
+    def transform(b, t):
         j = place[t]
-        x = jnp.concatenate([got[b, c, :, t].reshape(pulses, GB) for c in range(2)], axis=1)
-        for e, y in enumerate((x[:half] + x[half:], x[:half] - x[half:])):
-            high, low = parts(y)
-            rhs[e, 0:half] = high
-            rhs[e, half:2 * half] = low
-            rhs[e, 2 * half:] = high
-        for e in range(2):
-            lhs = jnp.concatenate([table[e, 0], table[e, 0], table[e, 1]], axis=1)
-            spec = dot(lhs, rhs[e])
-            re = spec[:half, :GB] + spec[half:, GB:]
-            im = spec[:half, GB:] - spec[half:, :GB]
-            p = re * re + im * im
+        for e, (high, low) in enumerate(branches(b, t)):
+            rhs[e, 0] = high
+            rhs[e, 1] = low
+        for e in range(RADIX):
+            p = intensity(table.at[e], rhs[e, 0], rhs[e, 1])
             power[b, j, e] = p
-            total = sums(b, p)
+            total = sums(p, band[b])
             own[b, j, e] = total[:, :GB]
             cross[b, j + 1, e] = total[:, GB:]
-            if final:
-                over[e] = total[:, GB:]
-                num[0, e] = p * scaled(b)
-                den[0, e] = total[:, :GB] + den[0, e]
 
     def scaled(b):
         return 2.0 * train[b].astype(jnp.float32)
 
     def lower():
-        return lax.broadcasted_iota(jnp.int32, (half, GB), 1) < GB // 2
+        return lax.broadcasted_iota(jnp.int32, (part, GB), 1) < GB // 2
 
     def ratio(b, j, e):
         total = own[b, j, e] + jnp.where(lower(), cross[b, j, e], cross[b, j + 2, e])
-        out.at[b, j][pl.ds(e, half, stride=2), :] = (
+        out.at[b, j][pl.ds(e, part, stride=RADIX), :] = (
             power[b, j, e] * scaled(b) / (floor[b] * scaled(b) + total)
         )
 
@@ -306,16 +323,16 @@
         den[0, e] = jnp.where(lower(), cross[b, pending[0], e], cross[b, pending[0] + 2, e]) + base
         for i, j in enumerate(pending[1:], 1):
             num[i, e] = power[b, j, e] * scaled(b)
-            part = jnp.where(lower(), cross[b, j, e], 0.0) if j < pending[0] else jnp.where(lower(), 0.0, cross[b, j + 2, e])
-            den[i, e] = own[b, j, e] + part + base
+            beside = cross[b, j, e] if j < pending[0] else cross[b, j + 2, e]
+            den[i, e] = own[b, j, e] + jnp.where(lower() == (j < pending[0]), beside, 0.0) + base
 
     def send_edges(b):
         for side in range(2):
             cut = slice(0, EDGE) if side == 0 else slice(GB - EDGE, GB)
-            for e in range(2):
+            for e in range(RADIX):
                 x = power[b, (tiles - 1) * side, e].T[cut]
-                for i in range(half // GB):
-                    start = (e * (half // GB) + i) * EDGE
+                for i in range(part // GB):
+                    start = (e * (part // GB) + i) * EDGE
                     edge[b, side, start:start + EDGE] = x[:, i * GB:(i + 1) * GB]
             pltpu.make_async_remote_copy(
                 src_ref=edge.at[b, side],
@@ -329,17 +346,17 @@
     def take_edges():
         pltpu.make_async_copy(edge, edge, edge_send).wait()
         pltpu.make_async_copy(halo, halo, edge_recv).wait()
-        zeros = jnp.zeros((GB - 2 * EDGE, half), jnp.float32)
+        zeros = jnp.zeros((GB - 2 * EDGE, part), jnp.float32)
 
         def lines(b, side, e):
-            start = [(e * (half // GB) + i) * EDGE for i in range(half // GB)]
+            start = [(e * (part // GB) + i) * EDGE for i in range(part // GB)]
             x = jnp.concatenate([halo[b, side, i:i + EDGE] for i in start], axis=1)
             return jnp.where(me > 0 if side else me < n - 1, x, 0.0)
 
         for b in range(beams):
-            for e in range(2):
+            for e in range(RADIX):
                 x = jnp.concatenate([lines(b, 0, e), zeros, lines(b, 1, e)], axis=0).T
-                total = sums(b, x)[:, GB:]
+                total = sums(x, band[b])[:, GB:]
                 cross[b, 0, e] = total
                 cross[b, tiles + 1, e] = total
 
@@ -358,14 +375,14 @@
 
     done = [set() for _ in range(beams)]
 
-    def ratios(b, ready, e):
+    def ratios(b, ready):
         for j in range(tiles):
             if b == beams - 1 and j in pending:
                 continue
             if j not in done[b] and {j - 1, j, j + 1} & set(range(tiles)) <= ready:
-                ratio(b, j, e)
-                if e == 1:
-                    done[b].add(j)
+                for e in range(RADIX):
+                    ratio(b, j, e)
+                done[b].add(j)
 
     for t in range(outer, tiles):
         ready = set(place[:t + 1])
@@ -374,34 +391,39 @@
             if final:
                 if t == outer:
                     take_edges()
-                for e in range(2):
+                    for i in range(beams - 1):
+                        ratios(i, ready)
+                for e in range(RADIX):
                     prepare(b, e)
+                sieve[...] = band[b]
+                factor[...] = jnp.full(factor.shape, scaled(b))
             arrived = got.at[b, :, :, t]
             pltpu.make_async_copy(arrived, arrived, recv_sem.at[b, t - outer + 1]).wait()
-            transform(b, t, final)
-            if t == tiles - 1 and not final and t > outer:
-                for e in range(2):
-                    ratios(b, ready, e)
+            if final:
+                for e, (high, low) in enumerate(branches(b, t)):
+                    tail[e, 0] = high
+                    tail[e, 1] = low
+                continue
+            transform(b, t)
+            if t == tiles - 1 and t > outer:
+                ratios(b, ready)
         if t == tiles - 2:
             take_edges()
             for b in range(beams):
-                for e in range(2):
-                    ratios(b, ready, e)
+                ratios(b, ready)
     if tiles == outer:
         take_edges()
-    if tiles <= outer + 1:
         for b in range(beams):
-            for e in range(2):
-                ratios(b, set(place), e)
+            ratios(b, set(place))
 
     whole = sent.at[:, :, :, pl.ds(0, (n - 1) * tiles)]
     pltpu.make_async_copy(whole, whole, send_sem).wait()
 
 
-def write_kernel(ratio, num, den, over, out, late, sem):
+def write_kernel(ratio, num, den, tail, table, sieve, factor, out, late, pw, sem):
     beams, tiles = ratio.shape[:2]
     pending = waiting(tiles)
-    half = num.shape[2]
+    part = num.shape[2]
 
     def put(b, j):
         i = pending.index(j) if b == beams - 1 and j in pending else None
@@ -412,13 +434,22 @@
         for j in range(tiles):
             if b < beams - 1 or j not in pending:
                 put(b, j).start()
-    lower = lax.broadcasted_iota(jnp.int32, (half, GB), 1) < GB // 2
-    for i, j in enumerate(pending):
-        for e in range(2):
-            total = den[i, e]
-            if i:
-                total += jnp.where(lower == (j > pending[0]), over[e], 0.0)
-            late.at[i][pl.ds(e, half, stride=2), :] = num[i, e] / total
+    lower = lax.broadcasted_iota(jnp.int32, (part, GB), 1) < GB // 2
+    if pending:
+        for e in range(RADIX):
+            pw[e] = intensity(table.at[e], tail[e, 0], tail[e, 1])
+
+        for e in range(RADIX):
+            p = pw[e]
+            total = sums(p, sieve[...])
+            for i, j in enumerate(pending):
+                if i:
+                    add = jnp.where(lower == (j > pending[0]), total[:, GB:], 0.0)
+                else:
+                    add = total[:, :GB]
+                top = num[i, e] if i else p * factor[0:1]
+                late.at[i][pl.ds(e, part, stride=RADIX), :] = top / (den[i, e] + add)
+    for j in pending:
         put(beams - 1, j).start()
     pltpu.make_async_copy(ratio, ratio, sem).wait()
 
@@ -432,7 +463,7 @@
         ga = gates // GB
         tiles = ga // n
         groups = local // ROWS
-        half = pulses // 2
+        part = pulses // RADIX
         consts = tables(gates, pulses, n)
         chain, twiddle, _ = consts
         vmem = pl.BlockSpec(memory_space=pltpu.VMEM)
@@ -440,15 +471,20 @@
         f32, bf16, i32 = jnp.float32, jnp.bfloat16, jnp.int32
         dma = pltpu.SemaphoreType.DMA
         late = max(1, len(waiting(tiles)))
-        held = (
-            (beams, tiles, pulses, GB), (late, 2, half, GB), (late, 2, half, GB), (2, half, GB),
-        )
-        room = 65456 * 1024 - sum(4 * math.prod(shape) for shape in held)
+        held = [
+            pltpu.VMEM(*x)
+            for x in (
+                ((beams, tiles, pulses, GB), f32), ((late, RADIX, part, GB), f32),
+                ((late, RADIX, part, GB), f32), ((RADIX, 2, part, 2 * GB), bf16),
+                ((RADIX, 2, 2 * part, part), bf16), ((2 * GB, 2 * GB), bf16), ((8, GB), f32),
+            )
+        ]
+        room = 65456 * 1024 - sum(x.dtype.itemsize * math.prod(x.shape) for x in held)
         results = pl.pallas_call(
             functools.partial(kernel, n, beams, pulses, gates),
-            out_shape=tuple(pltpu.VMEM(shape, f32) for shape in held),
+            out_shape=tuple(held),
             in_specs=[hbm] * 9,
-            out_specs=(vmem,) * 4,
+            out_specs=(vmem,) * len(held),
             scratch_shapes=[
                 pltpu.VMEM((beams, 2, local, gates), f32),
                 pltpu.VMEM((2, ga * ROWS, GB), f32),
@@ -456,11 +492,10 @@
                 pltpu.VMEM((2, ga, GB), f32),
                 pltpu.VMEM((beams, 2, groups, ga, ROWS, GB), f32),
                 pltpu.VMEM((beams, 2, pulses // ROWS, tiles, ROWS, GB), f32),
-                pltpu.VMEM((2, 2, pulses, half), bf16),
-                pltpu.VMEM((2, 3 * half, 2 * GB), bf16),
-                pltpu.VMEM((beams, tiles, 2, half, GB), f32),
-                pltpu.VMEM((beams, tiles, 2, half, GB), f32),
-                pltpu.VMEM((beams, tiles + 2, 2, half, GB), f32),
+                pltpu.VMEM((RADIX, 2, part, 2 * GB), bf16),
+                pltpu.VMEM((beams, tiles, RADIX, part, GB), f32),
+                pltpu.VMEM((beams, tiles, RADIX, part, GB), f32),
+                pltpu.VMEM((beams, tiles + 2, RADIX, part, GB), f32),
                 pltpu.VMEM((beams, 2, pulses // GB * EDGE, GB), f32),
                 pltpu.VMEM((beams, 2, pulses // GB * EDGE, GB), f32),
                 pltpu.VMEM((beams, 2 * GB, 2 * GB), bf16),
@@ -488,10 +523,10 @@
         return pl.pallas_call(
             write_kernel,
             out_shape=jax.ShapeDtypeStruct((1, beams, pulses, tiles * GB), f32),
-            in_specs=[vmem] * 4,
+            in_specs=[vmem] * len(held),
             out_specs=hbm,
-            scratch_shapes=[pltpu.VMEM((late, pulses, GB), f32), dma],
-            compiler_params=pltpu.CompilerParams(vmem_limit_bytes=2048 * 1024),
+            scratch_shapes=[pltpu.VMEM((late, pulses, GB), f32), pltpu.VMEM((RADIX, part, GB), f32), dma],
+            compiler_params=pltpu.CompilerParams(vmem_limit_bytes=4096 * 1024),
         )(*results)
 
     in_specs = (

time: 99 us -> 98 us (0.990)
  Pallas kernels: 98.9 us -> 97.9 us
    pallas_call x1, Pallas kernels: 97.6 us -> 96.4 us  [step(): pl.pallas_call(functools.partial(kernel, n, beams, pulses, gates), out_sh...]
where the time goes in v4:
time: 98 us; the launch traced here: 97.9 us
  Pallas kernels  97.9 us (100%)
    pallas_call x1, Pallas kernels, step(): pl.pallas_call(functools.partial(kernel, n, beams, pulses, gates), out_sh...  96.4 us

profile of v4, /device:TPU:9, one launch (start us, length us, event | category | flops | bytes accessed | tf_op | source)
XLA Modules:
  0.0 97.9 jit_solution(12268834439811073119)
XLA Ops:
  0.0 96.4 %shard_map.91 = (f32[2,4,512,128]{3,2,1,0:T(8,128)S(1)}, f32[3,4,128,128]{3,2,1,0:T(8,128)S(1)}, f32[3,4,128,128]{3,2,1,0:T(8,128)S(1)}, bf16[4,2,128,256]{3,2,1...) custom-call(f32[1,2,2,32,8192]{4,3,2,1,0:T(8,128)} %echoes.1, ...), custom_call_target="tpu_custom_call" | custom-call | tf_op jit(solution)/shard_map/pallas_call | solution.py:483
  96.4 1.5 %shard_map.92 = f32[1,2,512,512]{3,2,1,0:T(8,128)} custom-call(f32[2,4,512,128]{3,2,1,0:T(8,128)S(1)} %get-tuple-element.12.ratio, f32[3,4,128,128]{3,2,1,0:T(8,128)S(1)} %get-tuple-element.13.num, f32[3,4,128,128]{3,2,1,0:T(8,128)S(1)} %get-tuple-element.14.den, bf16[4,2,128,256]{3,2,1,0:T(8,128)(2,1)S(1)} %get-tuple-element.15.tail, ...), custom_call_target="tpu_custom_call" | custom-call | tf_op jit(solution)/shard_map/pallas_call | solution.py:523

commit v5 on v4

--- a/solution.py
+++ b/solution.py
@@ -110,9 +110,9 @@
     echoes, waveform_hbm, taper_hbm, guard_hbm, train_hbm, floor_hbm,
     chain_hbm, twiddle_hbm, doppler_hbm,
     out, num, den, tail, table, sieve, factor,
-    xin, xs, wave, filt, sent, got, rhs, power, own, cross, edge, halo, band,
+    xin, xs, wave, filt, sent, got, rhs, power, own, cross, edge, halo, relay, band,
     waveform, taper, guard, train, floor, chain, twiddle,
-    in_sem, small_sem, send_sem, recv_sem, edge_send, edge_recv,
+    in_sem, small_sem, send_sem, recv_sem, edge_send, edge_recv, relay_sem,
 ):
     me = lax.axis_index("shard")
     ga = gates // GB
@@ -326,26 +326,65 @@
             beside = cross[b, j, e] if j < pending[0] else cross[b, j + 2, e]
             den[i, e] = own[b, j, e] + jnp.where(lower() == (j < pending[0]), beside, 0.0) + base
 
+    relayed = n >= 8
+    relays = (side + 2, side - 3)
+    side_of = (side, side - 1)
+
+    def edge_copy(src, dst, to, send, recv):
+        return pltpu.make_async_remote_copy(
+            src_ref=src, dst_ref=dst, send_sem=send, recv_sem=recv,
+            device_id={"shard": to}, device_id_type=MESH,
+        )
+
     def send_edges(b):
-        for side in range(2):
-            cut = slice(0, EDGE) if side == 0 else slice(GB - EDGE, GB)
+        for way in range(2):
+            cut = slice(0, EDGE) if way == 0 else slice(GB - EDGE, GB)
             for e in range(RADIX):
-                x = power[b, (tiles - 1) * side, e].T[cut]
+                x = power[b, (tiles - 1) * way, e].T[cut]
                 for i in range(part // GB):
                     start = (e * (part // GB) + i) * EDGE
-                    edge[b, side, start:start + EDGE] = x[:, i * GB:(i + 1) * GB]
-            pltpu.make_async_remote_copy(
-                src_ref=edge.at[b, side],
-                dst_ref=halo.at[b, side],
-                send_sem=edge_send,
-                recv_sem=edge_recv,
-                device_id={"shard": lax.rem(me + (n - 1 if side == 0 else 1), n)},
-                device_id_type=MESH,
-            ).start()
+                    edge[b, way, start:start + EDGE] = x[:, i * GB:(i + 1) * GB]
+            border = side_of[way]
+            outside = me == (n - 1) * way
+            if b == 0 and relayed:
+                turn = me == border
+
+                @pl.when(turn)
+                def _():
+                    edge_copy(edge.at[b, way], relay, relays[way], edge_send.at[way], relay_sem.at[0]).start()
+
+                outside |= turn
+
+            @pl.when(jnp.logical_not(outside))
+            def _():
+                to = lax.rem(me + (1 if way else n - 1), n)
+                edge_copy(edge.at[b, way], halo.at[b, way], to, edge_send.at[way], edge_recv.at[way]).start()
+
+    def relay_copy(way):
+        to = side_of[1 - way]
+        return edge_copy(relay, halo.at[0, way], to, relay_sem.at[1], edge_recv.at[way])
+
+    def pass_edges():
+        for way in range(2 if relayed else 0):
+            @pl.when(me == relays[way])
+            def _():
+                pltpu.make_async_copy(relay, relay, relay_sem.at[0]).wait()
+                relay_copy(way).start()
+
+    def end_edges():
+        for way in range(2 if relayed else 0):
+            @pl.when(me == relays[way])
+            def _():
+                pltpu.make_async_copy(relay, relay, relay_sem.at[1]).wait()
 
     def take_edges():
-        pltpu.make_async_copy(edge, edge, edge_send).wait()
-        pltpu.make_async_copy(halo, halo, edge_recv).wait()
+        for way in range(2):
+            @pl.when(me != (n - 1) * way)
+            def _():
+                gone, come = edge.at[:, way], halo.at[:, 1 - way]
+                pltpu.make_async_copy(gone, gone, edge_send.at[way]).wait()
+                pltpu.make_async_copy(come, come, edge_recv.at[1 - way]).wait()
+
         zeros = jnp.zeros((GB - 2 * EDGE, part), jnp.float32)
 
         def lines(b, side, e):
@@ -367,6 +406,7 @@
             transform(b, t)
         send_edges(b)
 
+    pass_edges()
     if tiles > outer:
         for b in range(beams):
             send_slot(b, tiles - 1, near, True)
@@ -416,6 +456,7 @@
         for b in range(beams):
             ratios(b, set(place))
 
+    end_edges()
     whole = sent.at[:, :, :, pl.ds(0, (n - 1) * tiles)]
     pltpu.make_async_copy(whole, whole, send_sem).wait()
 
@@ -498,6 +539,7 @@
                 pltpu.VMEM((beams, tiles + 2, RADIX, part, GB), f32),
                 pltpu.VMEM((beams, 2, pulses // GB * EDGE, GB), f32),
                 pltpu.VMEM((beams, 2, pulses // GB * EDGE, GB), f32),
+                pltpu.VMEM((pulses // GB * EDGE, GB), f32),
                 pltpu.VMEM((beams, 2 * GB, 2 * GB), bf16),
                 pltpu.VMEM((2, gates), f32),
                 pltpu.SMEM((pulses,), f32),
@@ -510,8 +552,9 @@
                 dma((4,)),
                 dma,
                 dma((beams, tiles - min(2, tiles) + 1)),
-                dma,
-                dma,
+                dma((2,)),
+                dma((2,)),
+                dma((2,)),
             ],
             compiler_params=pltpu.CompilerParams(
                 collective_id=0, has_side_effects=True, vmem_limit_bytes=room

time: 98 us -> 97.6 us (level)
  no operation moved by 1% of the time
where the time goes in v5:
time: 97.6 us; the launch traced here: 97.5 us
  Pallas kernels  97.5 us (100%)
    pallas_call x1, Pallas kernels, step(): pl.pallas_call(functools.partial(kernel, n, beams, pulses, gates), out_sh...  96 us

profile of v5, /device:TPU:9, one launch (start us, length us, event | category | flops | bytes accessed | tf_op | source)
XLA Modules:
  0.0 97.5 jit_solution(2303122899410615691)
XLA Ops:
  0.0 96.0 %shard_map.91 = (f32[2,4,512,128]{3,2,1,0:T(8,128)S(1)}, f32[3,4,128,128]{3,2,1,0:T(8,128)S(1)}, f32[3,4,128,128]{3,2,1,0:T(8,128)S(1)}, bf16[4,2,128,256]{3,2,1...) custom-call(f32[1,2,2,32,8192]{4,3,2,1,0:T(8,128)} %echoes.1, ...), custom_call_target="tpu_custom_call" | custom-call | tf_op jit(solution)/shard_map/pallas_call | solution.py:524
  96.0 1.5 %shard_map.92 = f32[1,2,512,512]{3,2,1,0:T(8,128)} custom-call(f32[2,4,512,128]{3,2,1,0:T(8,128)S(1)} %get-tuple-element.12.ratio, f32[3,4,128,128]{3,2,1,0:T(8,128)S(1)} %get-tuple-element.13.num, f32[3,4,128,128]{3,2,1,0:T(8,128)S(1)} %get-tuple-element.14.den, bf16[4,2,128,256]{3,2,1,0:T(8,128)(2,1)S(1)} %get-tuple-element.15.tail, ...), custom_call_target="tpu_custom_call" | custom-call | tf_op jit(solution)/shard_map/pallas_call | solution.py:566

commit v6 on v5

--- a/solution.py
+++ b/solution.py
@@ -87,6 +87,11 @@
     sr, si, tr, ti = ar + cr, ai + ci, ar - cr, ai - ci
     ur, ui, vr, vi = br + dr, bi + di, br - dr, bi - di
     return [(sr + ur, si + ui), (tr + vi, ti - vr), (sr - ur, si - ui), (tr - vi, ti + vr)]
+
+
+def branches(re, im):
+    x = [y.reshape(RADIX, -1, GB) for y in (re, im)]
+    return [parts(jnp.concatenate(y, axis=1)) for y in rotated([(x[0][i], x[1][i]) for i in range(RADIX)])]
 
 
 def stacked(high, low, axis):
@@ -240,7 +245,7 @@
     def send_slot(b, t, peers, keep):
         send(
             lambda to: sent.at[b, :, :, to * tiles + t],
-            got.at[b, :, pl.ds(me * groups, groups), t],
+            tail.at[:, pl.ds(me * groups, groups)] if (b, t) == (beams - 1, tiles - 1) else got.at[b, :, pl.ds(me * groups, groups), t],
             recv_sem.at[b, t - outer + 1], peers, keep,
         )
 
@@ -290,13 +295,9 @@
 
     pending = waiting(tiles)
 
-    def branches(b, t):
-        x = [got[b, c, :, t].reshape(RADIX, part, GB) for c in range(2)]
-        return [parts(jnp.concatenate(y, axis=1)) for y in rotated([(x[0][i], x[1][i]) for i in range(RADIX)])]
-
     def transform(b, t):
         j = place[t]
-        for e, (high, low) in enumerate(branches(b, t)):
+        for e, (high, low) in enumerate(branches(got[b, 0, :, t], got[b, 1, :, t])):
             rhs[e, 0] = high
             rhs[e, 1] = low
         for e in range(RADIX):
@@ -437,12 +438,9 @@
                     prepare(b, e)
                 sieve[...] = band[b]
                 factor[...] = jnp.full(factor.shape, scaled(b))
-            arrived = got.at[b, :, :, t]
+            arrived = tail if final else got.at[b, :, :, t]
             pltpu.make_async_copy(arrived, arrived, recv_sem.at[b, t - outer + 1]).wait()
             if final:
-                for e, (high, low) in enumerate(branches(b, t)):
-                    tail[e, 0] = high
-                    tail[e, 1] = low
                 continue
             transform(b, t)
             if t == tiles - 1 and t > outer:
@@ -461,7 +459,7 @@
     pltpu.make_async_copy(whole, whole, send_sem).wait()
 
 
-def write_kernel(ratio, num, den, tail, table, sieve, factor, out, late, pw, sem):
+def write_kernel(ratio, num, den, tail, table, sieve, factor, out, late, pw, split_in, sem):
     beams, tiles = ratio.shape[:2]
     pending = waiting(tiles)
     part = num.shape[2]
@@ -477,8 +475,11 @@
                 put(b, j).start()
     lower = lax.broadcasted_iota(jnp.int32, (part, GB), 1) < GB // 2
     if pending:
+        for e, (high, low) in enumerate(branches(tail[0], tail[1])):
+            split_in[e, 0] = high
+            split_in[e, 1] = low
         for e in range(RADIX):
-            pw[e] = intensity(table.at[e], tail[e, 0], tail[e, 1])
+            pw[e] = intensity(table.at[e], split_in[e, 0], split_in[e, 1])
 
         for e in range(RADIX):
             p = pw[e]
@@ -516,7 +517,7 @@
             pltpu.VMEM(*x)
             for x in (
                 ((beams, tiles, pulses, GB), f32), ((late, RADIX, part, GB), f32),
-                ((late, RADIX, part, GB), f32), ((RADIX, 2, part, 2 * GB), bf16),
+                ((late, RADIX, part, GB), f32), ((2, pulses // ROWS, ROWS, GB), f32),
                 ((RADIX, 2, 2 * part, part), bf16), ((2 * GB, 2 * GB), bf16), ((8, GB), f32),
             )
         ]
@@ -568,7 +569,7 @@
             out_shape=jax.ShapeDtypeStruct((1, beams, pulses, tiles * GB), f32),
             in_specs=[vmem] * len(held),
             out_specs=hbm,
-            scratch_shapes=[pltpu.VMEM((late, pulses, GB), f32), pltpu.VMEM((RADIX, part, GB), f32), dma],
+            scratch_shapes=[pltpu.VMEM((late, pulses, GB), f32), pltpu.VMEM((RADIX, part, GB), f32), pltpu.VMEM((RADIX, 2, part, 2 * GB), bf16), dma],
             compiler_params=pltpu.CompilerParams(vmem_limit_bytes=4096 * 1024),
         )(*results)
 

time: 97.6 us -> 97.5 us (level)
  no operation moved by 1% of the time
where the time goes in v6:
time: 97.5 us; the launch traced here: 97.4 us
  Pallas kernels  97.4 us (100%)
    pallas_call x1, Pallas kernels, step(): pl.pallas_call(functools.partial(kernel, n, beams, pulses, gates), out_sh...  95.9 us

profile of v6, /device:TPU:9, one launch (start us, length us, event | category | flops | bytes accessed | tf_op | source)
XLA Modules:
  0.0 97.4 jit_solution(16191921524142921016)
XLA Ops:
  0.0 95.9 %shard_map.91 = (f32[2,4,512,128]{3,2,1,0:T(8,128)S(1)}, f32[3,4,128,128]{3,2,1,0:T(8,128)S(1)}, f32[3,4,128,128]{3,2,1,0:T(8,128)S(1)}, f32[2,64,8,128]{3,2,1,0...) custom-call(f32[1,2,2,32,8192]{4,3,2,1,0:T(8,128)} %echoes.1, ...), custom_call_target="tpu_custom_call" | custom-call | tf_op jit(solution)/shard_map/pallas_call | solution.py:525
  95.9 1.5 %shard_map.92 = f32[1,2,512,512]{3,2,1,0:T(8,128)} custom-call(f32[2,4,512,128]{3,2,1,0:T(8,128)S(1)} %get-tuple-element.12.ratio, f32[3,4,128,128]{3,2,1,0:T(8,128)S(1)} %get-tuple-element.13.num, f32[3,4,128,128]{3,2,1,0:T(8,128)S(1)} %get-tuple-element.14.den, f32[2,64,8,128]{3,2,1,0:T(8,128)S(1)} %get-tuple-element.15.tail, ...), custom_call_target="tpu_custom_call" | custom-call | tf_op jit(solution)/shard_map/pallas_call | solution.py:567
